TPU v7x, 32 devices: a whole 2x2x4 slice. The times are simulated.
32 devices in a mesh: expert: 4 (over y, core), shard: 8 (over z, x).
Axes of the slice: x: 2, y: 2, z: 4, core: 2. Of those that a mesh axis runs over, the one named last changes fastest.
Arguments:
- hidden_in: bfloat16 [12288, 1536], P(('expert', 'shard')), may hold values from -6 to 6
- cotangent: bfloat16 [12288, 1536], P(('expert', 'shard')), may hold values from -6 to 6
- routes: int32 [12288, 8], P(('expert', 'shard')), may hold values from 0 to 19, all different within a row; in each aligned block of 384 rows (0 to 383, 384 to 767, ...) at most 256 rows name the same one
- attn_gain: bfloat16 [1536], P('shard'), may hold values from 0.5 to 1.5
- q_weight: bfloat16 [1536, 1536], P('shard'), may hold values from -0.21875 to 0.21875
- k_weight: bfloat16 [1536, 512], P('shard'), may hold values from -0.21875 to 0.21875
- v_weight: bfloat16 [1536, 512], P('shard'), may hold values from -0.15625 to 0.15625
- o_weight: bfloat16 [1536, 1536], P('shard'), may hold values from -1 to 1
- ffn_gain: bfloat16 [1536], P('shard'), may hold values from 0.5 to 1.5
- router_weight: bfloat16 [1536, 20], P('shard'), may hold values from -0.078125 to 0.078125
- gate_weight: bfloat16 [20, 1536, 512], P('expert', 'shard'), may hold values from -0.15625 to 0.15625
- up_weight: bfloat16 [20, 1536, 512], P('expert', 'shard'), may hold values from -0.15625 to 0.15625
- down_weight: bfloat16 [20, 512, 1536], P('expert', 'shard'), may hold values from -1.5 to 1.5
Outputs:
- hidden_out: bfloat16 [12288, 1536], P(('expert', 'shard'))
- grad_hidden: bfloat16 [12288, 1536], P(('expert', 'shard'))
- grad_attn_gain: float32 [1536], P('shard')
- grad_q: float32 [1536, 1536], P('shard')
- grad_k: float32 [1536, 512], P('shard')
- grad_v: float32 [1536, 512], P('shard')
- grad_o: float32 [1536, 1536], P('shard')
- grad_ffn_gain: float32 [1536], P('shard')
- grad_router: float32 [1536, 20], P('shard')
- grad_gate: float32 [20, 1536, 512], P('expert', 'shard')
- grad_up: float32 [20, 1536, 512], P('expert', 'shard')
- grad_down: float32 [20, 512, 1536], P('expert', 'shard')
Inputs may be any that keep to these rules, and one draw needn't show every extreme that they name: In the 384 rows of one device no expert is named by more than 256 routes, and in every draw some expert is named by exactly 256 there; the routes of a row are distinct.
All inputs are finite; a program needn't handle non-finite values.
Results may differ from a plain program's by a relative error of at most 0.025.
Values may be sent and summed in bfloat16 or wider, within the bound.
A program may use at most 320 MiB of HBM per device.

v0:
```python
import jax
import jax.numpy as jnp
from jax import lax
from jax.sharding import PartitionSpec as P

HS = 64
PR_DEV = 128


epsilon = 1e-05
negative = -1e30


def swapped(block, axis, apart):
    count = lax.axis_size(axis)
    route = []
    for low in range(count):
        high = low | 1 << apart
        if high != low and high < count:
            route += [(low, high), (high, low)]
    return lax.ppermute(block, axis, route)


def rotate_half(values):
    middle = values.shape[-1] // 2
    return jnp.concatenate([-values[..., middle:], values[..., :middle]], -1)


def rope_tables(positions, head_size):
    inv_freq = 10000.0 ** (-jnp.arange(head_size // 2, dtype=jnp.float32) * 2.0 / head_size)
    angles = positions.astype(jnp.float32)[:, None] * inv_freq[None, :]
    angles = jnp.concatenate([angles, angles], -1)
    return (jnp.cos(angles), jnp.sin(angles))


def rope_apply(values, cosine_table, sine_table):
    return values * cosine_table[:, None, :] + rotate_half(values) * sine_table[:, None, :]


def rope_revert(gradient, cosine_table, sine_table):
    return gradient * cosine_table[:, None, :] - rotate_half(gradient * sine_table[:, None, :])


def norm_rows(values, gain_row):
    inverse = lax.rsqrt(jnp.mean(values * values, -1, keepdims=True) + epsilon)
    normed = values * inverse
    return (normed, inverse, normed * gain_row.astype(jnp.float32))


def norm_back(grad_out, normed, inverse, gain_row):
    scaled = grad_out * gain_row.astype(jnp.float32)
    grad_in = inverse * (scaled - normed * jnp.mean(scaled * normed, -1, keepdims=True))
    return (grad_in, jnp.sum(grad_out * normed, 0))


def head_scores(query_head, key_head, allowed, score_scale):
    scores = (
        jnp.einsum("tgs,ks->gtk", query_head, key_head, preferred_element_type=jnp.float32)
        * score_scale
    )
    return jnp.where(allowed[None], scores, negative)


def head_forward(query_head, key_head, value_head, allowed, score_scale):
    scores = head_scores(query_head, key_head, allowed, score_scale)
    row_max = jnp.max(scores, -1, keepdims=True)
    exp_scores = jnp.exp(scores - row_max)
    row_total = jnp.sum(exp_scores, -1, keepdims=True)
    attn_probs = (exp_scores / row_total).astype(jnp.bfloat16)
    head_out = jnp.einsum("gtk,ks->tgs", attn_probs, value_head, preferred_element_type=jnp.float32)
    return (head_out.astype(jnp.bfloat16), (row_max + jnp.log(row_total))[..., 0])


def head_backward(query_head, key_head, value_head, grad_head, log_total, allowed, score_scale):
    scores = head_scores(query_head, key_head, allowed, score_scale)
    attn_probs = jnp.exp(scores - log_total[..., None])
    grad_value = jnp.einsum(
        "gtk,tgs->ks",
        attn_probs.astype(jnp.bfloat16),
        grad_head,
        preferred_element_type=jnp.float32,
    )
    grad_probs = jnp.einsum(
        "tgs,ks->gtk", grad_head, value_head, preferred_element_type=jnp.float32
    )
    row_delta = jnp.sum(attn_probs * grad_probs, -1, keepdims=True)
    grad_scores = (attn_probs * (grad_probs - row_delta)).astype(jnp.bfloat16)
    grad_query = (
        jnp.einsum("gtk,ks->tgs", grad_scores, key_head, preferred_element_type=jnp.float32)
        * score_scale
    )
    grad_key = (
        jnp.einsum("gtk,tgs->ks", grad_scores, query_head, preferred_element_type=jnp.float32)
        * score_scale
    )
    return (grad_query, grad_key, grad_value)


def body(
    hidden_in,
    cotangent,
    routes,
    attn_gain,
    q_weight,
    k_weight,
    v_weight,
    o_weight,
    ffn_gain,
    router_weight,
    gate_weight,
    up_weight,
    down_weight,
):
    gathered = (
        lax.all_gather(attn_gain, "shard", axis=0, tiled=True),
        lax.all_gather(q_weight, "shard", axis=0, tiled=True),
        lax.all_gather(k_weight, "shard", axis=0, tiled=True),
        lax.all_gather(v_weight, "shard", axis=0, tiled=True),
        lax.all_gather(o_weight, "shard", axis=0, tiled=True),
        lax.all_gather(ffn_gain, "shard", axis=0, tiled=True),
        lax.all_gather(router_weight, "shard", axis=0, tiled=True),
        lax.all_gather(gate_weight, "shard", axis=1, tiled=True),
        lax.all_gather(up_weight, "shard", axis=1, tiled=True),
        lax.all_gather(down_weight, "shard", axis=1, tiled=True),
    )
    gain_one, w_query, w_key, w_value, w_out, gain_two, w_router, w_gate, w_up, w_down = gathered
    tok_rows = hidden_in.shape[0]
    model_width = hidden_in.shape[1]
    shards = lax.axis_size("shard")
    groups = lax.axis_size("expert")
    experts_here = gate_weight.shape[0]
    experts_all = router_weight.shape[1]
    top_k = routes.shape[1]
    half_len = tok_rows - PR_DEV
    prompt_len = PR_DEV * shards
    key_count = prompt_len + 2 * half_len
    capacity = tok_rows * top_k * 5 // (3 * experts_all)
    slot_total = experts_all * capacity
    heads_q = w_query.shape[1] // HS
    heads_kv = w_key.shape[1] // HS
    group_size = heads_q // heads_kv
    score_scale = HS ** (-0.5)
    shard_pos = lax.axis_index("shard")
    odd_half = shard_pos % 2
    row_index = jnp.arange(tok_rows, dtype=jnp.int32)
    cont_row = row_index - PR_DEV
    prompt_row = row_index < PR_DEV
    global_row = shard_pos * PR_DEV + row_index
    positions = jnp.where(prompt_row, global_row, prompt_len + 2 * cont_row + odd_half)
    cosine_table, sine_table = rope_tables(positions, HS)
    key_index = jnp.arange(key_count, dtype=jnp.int32)
    prompt_key = key_index < prompt_len
    partner_col = key_index - prompt_len
    partner_key = (partner_col >= 0) & (partner_col < half_len)
    own_col = key_index - prompt_len - half_len
    allowed = jnp.where(
        prompt_row[:, None],
        prompt_key[None, :] & (key_index[None, :] <= global_row[:, None]),
        prompt_key[None, :]
        | partner_key[None, :] & (partner_col[None, :] < cont_row[:, None] + odd_half)
        | (own_col[None, :] >= 0) & (own_col[None, :] <= cont_row[:, None]),
    )
    x_float = hidden_in.astype(jnp.float32)
    normed_one, inverse_one, scaled_one = norm_rows(x_float, gain_one)
    attn_input = scaled_one.astype(jnp.bfloat16)
    query_lin = jnp.dot(attn_input, w_query, preferred_element_type=jnp.float32)
    key_lin = jnp.dot(attn_input, w_key, preferred_element_type=jnp.float32)
    value_lin = jnp.dot(attn_input, w_value, preferred_element_type=jnp.float32)
    queries = rope_apply(query_lin.reshape(tok_rows, heads_q, HS), cosine_table, sine_table).astype(
        jnp.bfloat16
    )
    key_rows = rope_apply(key_lin.reshape(tok_rows, heads_kv, HS), cosine_table, sine_table).astype(
        jnp.bfloat16
    )
    key_rows = key_rows.reshape(tok_rows, heads_kv * HS)
    value_rows = value_lin.astype(jnp.bfloat16)
    prompt_keys, prompt_values = (
        lax.all_gather(key_rows[:PR_DEV], "shard", axis=0, tiled=True),
        lax.all_gather(value_rows[:PR_DEV], "shard", axis=0, tiled=True),
    )
    partner_keys, partner_values = swapped((key_rows[PR_DEV:], value_rows[PR_DEV:]), "shard", 0)
    all_keys = jnp.concatenate([prompt_keys, partner_keys, key_rows[PR_DEV:]], 0)
    all_values = jnp.concatenate([prompt_values, partner_values, value_rows[PR_DEV:]], 0)
    query_heads = jnp.moveaxis(queries.reshape(tok_rows, heads_kv, group_size, HS), 1, 0)
    key_heads = jnp.moveaxis(all_keys.reshape(key_count, heads_kv, HS), 1, 0)
    value_heads = jnp.moveaxis(all_values.reshape(key_count, heads_kv, HS), 1, 0)

    def forward_head(operands):
        return head_forward(operands[0], operands[1], operands[2], allowed, score_scale)

    head_outs, head_totals = lax.map(forward_head, (query_heads, key_heads, value_heads))
    attn_mix = jnp.moveaxis(head_outs, 0, 1).reshape(tok_rows, heads_q * HS)
    residual = x_float + jnp.dot(attn_mix, w_out, preferred_element_type=jnp.float32)
    normed_two, inverse_two, scaled_two = norm_rows(residual, gain_two)
    ffn_input = scaled_two.astype(jnp.bfloat16)
    logits = jnp.dot(ffn_input, w_router, preferred_element_type=jnp.float32)
    expert_ids = jnp.arange(experts_all, dtype=jnp.int32)
    chosen = (routes[:, :, None] == expert_ids[None, None, :]).astype(jnp.float32)
    route_gates = jax.nn.softmax(jnp.sum(chosen * logits[:, None, :], -1), -1)
    flat_routes = routes.reshape(-1)
    route_count = flat_routes.shape[0]
    route_hits = (flat_routes[:, None] == expert_ids[None, :]).astype(jnp.int32)
    slot_index = jnp.sum((jnp.cumsum(route_hits, 0) - 1) * route_hits, 1)
    destination = flat_routes * capacity + slot_index
    slot_route = (
        jnp.zeros(slot_total, jnp.int32)
        .at[destination]
        .set(jnp.arange(route_count, dtype=jnp.int32))
    )
    slot_used = jnp.zeros(slot_total, jnp.bool_).at[destination].set(True)
    slot_token = slot_route // top_k
    zero_value = jnp.zeros((), jnp.bfloat16)
    outgoing = jnp.where(slot_used[:, None], ffn_input[slot_token], zero_value)
    incoming = lax.all_to_all(
        outgoing.reshape(groups, experts_here, capacity, model_width),
        "expert",
        split_axis=0,
        concat_axis=0,
        tiled=True,
    )
    gate_proj = jnp.einsum("sxcd,xdf->xscf", incoming, w_gate, preferred_element_type=jnp.float32)
    up_proj = jnp.einsum("sxcd,xdf->xscf", incoming, w_up, preferred_element_type=jnp.float32)
    sig_gate = jax.nn.sigmoid(gate_proj)
    silu_gate = gate_proj * sig_gate
    inner_act = (silu_gate * up_proj).astype(jnp.bfloat16)
    expert_out = jnp.einsum(
        "xscf,xfd->sxcd", inner_act, w_down, preferred_element_type=jnp.float32
    ).astype(jnp.bfloat16)
    returned = lax.all_to_all(
        expert_out, "expert", split_axis=0, concat_axis=0, tiled=True
    ).reshape(slot_total, model_width)
    route_out = returned[destination].reshape(tok_rows, top_k, model_width)
    mixture = jnp.sum(route_out.astype(jnp.float32) * route_gates[:, :, None], 1)
    hidden_out = (residual + mixture).astype(jnp.bfloat16)
    grad_y = cotangent.astype(jnp.float32)
    grad_gates = jnp.sum(route_out.astype(jnp.float32) * grad_y[:, None, :], -1)
    grad_route = (
        (route_gates[:, :, None] * grad_y[:, None, :])
        .astype(jnp.bfloat16)
        .reshape(route_count, model_width)
    )
    grad_slots = jnp.where(slot_used[:, None], grad_route[slot_route], zero_value)
    grad_back = lax.all_to_all(
        grad_slots.reshape(groups, experts_here, capacity, model_width),
        "expert",
        split_axis=0,
        concat_axis=0,
        tiled=True,
    )
    grad_inner = jnp.einsum("sxcd,xfd->xscf", grad_back, w_down, preferred_element_type=jnp.float32)
    term_down = jnp.einsum(
        "xscf,sxcd->xfd", inner_act, grad_back, preferred_element_type=jnp.float32
    )
    grad_gate_proj = (
        grad_inner * up_proj * sig_gate * (1.0 + gate_proj * (1.0 - sig_gate))
    ).astype(jnp.bfloat16)
    grad_up_proj = (grad_inner * silu_gate).astype(jnp.bfloat16)
    term_gate = jnp.einsum(
        "sxcd,xscf->xdf", incoming, grad_gate_proj, preferred_element_type=jnp.float32
    )
    term_up = jnp.einsum(
        "sxcd,xscf->xdf", incoming, grad_up_proj, preferred_element_type=jnp.float32
    )
    grad_rows = (
        jnp.einsum("xscf,xdf->sxcd", grad_gate_proj, w_gate, preferred_element_type=jnp.float32)
        + jnp.einsum("xscf,xdf->sxcd", grad_up_proj, w_up, preferred_element_type=jnp.float32)
    ).astype(jnp.bfloat16)
    grad_arrived = lax.all_to_all(
        grad_rows, "expert", split_axis=0, concat_axis=0, tiled=True
    ).reshape(slot_total, model_width)
    grad_ffn_input = jnp.sum(
        grad_arrived[destination].reshape(tok_rows, top_k, model_width).astype(jnp.float32), 1
    )
    centered = grad_gates - jnp.sum(grad_gates * route_gates, -1, keepdims=True)
    grad_logits = jnp.sum(chosen * (route_gates * centered)[:, :, None], 1).astype(jnp.bfloat16)
    grad_ffn_input = grad_ffn_input + jnp.dot(
        grad_logits, w_router.T, preferred_element_type=jnp.float32
    )
    term_router = jnp.dot(ffn_input.T, grad_logits, preferred_element_type=jnp.float32)
    grad_resid_norm, term_gain_two = norm_back(grad_ffn_input, normed_two, inverse_two, gain_two)
    grad_residual = grad_y + grad_resid_norm
    grad_branch = grad_residual.astype(jnp.bfloat16)
    term_out = jnp.dot(attn_mix.T, grad_branch, preferred_element_type=jnp.float32)
    grad_mix = jnp.dot(grad_branch, w_out.T, preferred_element_type=jnp.float32).astype(
        jnp.bfloat16
    )
    grad_heads = jnp.moveaxis(grad_mix.reshape(tok_rows, heads_kv, group_size, HS), 1, 0)

    def backward_head(operands):
        return head_backward(
            operands[0], operands[1], operands[2], operands[3], operands[4], allowed, score_scale
        )

    grad_q_heads, grad_k_heads, grad_v_heads = lax.map(
        backward_head, (query_heads, key_heads, value_heads, grad_heads, head_totals)
    )
    grad_queries = jnp.moveaxis(grad_q_heads, 0, 1).reshape(tok_rows, heads_q, HS)
    grad_keys_all = jnp.moveaxis(grad_k_heads, 0, 1).reshape(key_count, heads_kv * HS)
    grad_values_all = jnp.moveaxis(grad_v_heads, 0, 1).reshape(key_count, heads_kv * HS)
    prompt_grad_k, prompt_grad_v = (
        lax.psum_scatter(
            grad_keys_all[:prompt_len].astype(jnp.bfloat16),
            "shard",
            scatter_dimension=0,
            tiled=True,
        ).astype(jnp.float32),
        lax.psum_scatter(
            grad_values_all[:prompt_len].astype(jnp.bfloat16),
            "shard",
            scatter_dimension=0,
            tiled=True,
        ).astype(jnp.float32),
    )
    partner_grad_k, partner_grad_v = (
        swapped(
            grad_keys_all[prompt_len : prompt_len + half_len].astype(jnp.bfloat16), "shard", 0
        ).astype(jnp.float32),
        swapped(
            grad_values_all[prompt_len : prompt_len + half_len].astype(jnp.bfloat16), "shard", 0
        ).astype(jnp.float32),
    )
    own_grad_k = jnp.concatenate(
        [prompt_grad_k, grad_keys_all[prompt_len + half_len :] + partner_grad_k], 0
    )
    own_grad_v = jnp.concatenate(
        [prompt_grad_v, grad_values_all[prompt_len + half_len :] + partner_grad_v], 0
    )
    grad_q_lin = (
        rope_revert(grad_queries, cosine_table, sine_table)
        .reshape(tok_rows, heads_q * HS)
        .astype(jnp.bfloat16)
    )
    grad_k_lin = (
        rope_revert(own_grad_k.reshape(tok_rows, heads_kv, HS), cosine_table, sine_table)
        .reshape(tok_rows, heads_kv * HS)
        .astype(jnp.bfloat16)
    )
    grad_v_lin = own_grad_v.astype(jnp.bfloat16)
    grad_attn_input = (
        jnp.dot(grad_q_lin, w_query.T, preferred_element_type=jnp.float32)
        + jnp.dot(grad_k_lin, w_key.T, preferred_element_type=jnp.float32)
        + jnp.dot(grad_v_lin, w_value.T, preferred_element_type=jnp.float32)
    )
    term_query = jnp.dot(attn_input.T, grad_q_lin, preferred_element_type=jnp.float32)
    term_key = jnp.dot(attn_input.T, grad_k_lin, preferred_element_type=jnp.float32)
    term_value = jnp.dot(attn_input.T, grad_v_lin, preferred_element_type=jnp.float32)
    grad_x_norm, term_gain_one = norm_back(grad_attn_input, normed_one, inverse_one, gain_one)
    grad_hidden = (grad_residual + grad_x_norm).astype(jnp.bfloat16)
    summed = (
        lax.psum_scatter(
            term_gain_one.astype(jnp.bfloat16), "shard", scatter_dimension=0, tiled=True
        ).astype(jnp.float32),
        lax.psum_scatter(
            term_query.astype(jnp.bfloat16), "shard", scatter_dimension=0, tiled=True
        ).astype(jnp.float32),
        lax.psum_scatter(
            term_key.astype(jnp.bfloat16), "shard", scatter_dimension=0, tiled=True
        ).astype(jnp.float32),
        lax.psum_scatter(
            term_value.astype(jnp.bfloat16), "shard", scatter_dimension=0, tiled=True
        ).astype(jnp.float32),
        lax.psum_scatter(
            term_out.astype(jnp.bfloat16), "shard", scatter_dimension=0, tiled=True
        ).astype(jnp.float32),
        lax.psum_scatter(
            term_gain_two.astype(jnp.bfloat16), "shard", scatter_dimension=0, tiled=True
        ).astype(jnp.float32),
        lax.psum_scatter(
            term_router.astype(jnp.bfloat16), "shard", scatter_dimension=0, tiled=True
        ).astype(jnp.float32),
        lax.psum_scatter(
            term_gate.astype(jnp.bfloat16), "shard", scatter_dimension=1, tiled=True
        ).astype(jnp.float32),
        lax.psum_scatter(
            term_up.astype(jnp.bfloat16), "shard", scatter_dimension=1, tiled=True
        ).astype(jnp.float32),
        lax.psum_scatter(
            term_down.astype(jnp.bfloat16), "shard", scatter_dimension=1, tiled=True
        ).astype(jnp.float32),
    )
    mixer_grads = (
        lax.psum(summed[0].astype(jnp.bfloat16), "expert").astype(jnp.float32),
        lax.psum(summed[1].astype(jnp.bfloat16), "expert").astype(jnp.float32),
        lax.psum(summed[2].astype(jnp.bfloat16), "expert").astype(jnp.float32),
        lax.psum(summed[3].astype(jnp.bfloat16), "expert").astype(jnp.float32),
        lax.psum(summed[4].astype(jnp.bfloat16), "expert").astype(jnp.float32),
        lax.psum(summed[5].astype(jnp.bfloat16), "expert").astype(jnp.float32),
        lax.psum(summed[6].astype(jnp.bfloat16), "expert").astype(jnp.float32),
    )
    expert_grads = (summed[7], summed[8], summed[9])
    return (
        hidden_out,
        grad_hidden,
        mixer_grads[0],
        mixer_grads[1],
        mixer_grads[2],
        mixer_grads[3],
        mixer_grads[4],
        mixer_grads[5],
        mixer_grads[6],
        expert_grads[0],
        expert_grads[1],
        expert_grads[2],
    )


def solution(mesh):
    return jax.shard_map(
        body,
        mesh=mesh,
        in_specs=(
            P(("expert", "shard"), None),
            P(("expert", "shard"), None),
            P(("expert", "shard"), None),
            P("shard"),
            P("shard", None),
            P("shard", None),
            P("shard", None),
            P("shard", None),
            P("shard"),
            P("shard", None),
            P("expert", "shard", None),
            P("expert", "shard", None),
            P("expert", "shard", None),
        ),
        out_specs=(
            P(("expert", "shard"), None),
            P(("expert", "shard"), None),
            P("shard"),
            P("shard", None),
            P("shard", None),
            P("shard", None),
            P("shard", None),
            P("shard"),
            P("shard", None),
            P("expert", "shard", None),
            P("expert", "shard", None),
            P("expert", "shard", None),
        ),
        check_vma=False,
    )
```

profile of v0, /device:TPU:0, one launch (start us, length us, event | category | flops | bytes accessed | tf_op | source)
XLA Modules:
  0.0 2453.7 jit_solution(5285527537657344404)
XLA Ops:
  12.4 23.5 all-reduce.5
  37.5 19.8 all-gather.11.cloned.1.call-done
  61.0 41.1 %all-gather.15.cloned.1.call-done = bf16[1536,512]{1,0:T(8,128)(2,1)} async-done(((bf16[192,512]{1,0:T(8,128)(2,1)}), bf16[1536,512]{1,0:T(8,128)(2,1)}) %all-gather.15.cloned.1.call-update) | async-done | bytes 1572880 | tf_op jit(solution)/shard_map/all_gather | solution.py:117
  121.3 30.7 %all-gather = bf16[8,192,20]{1,2,0:T(8,128)(2,1)S(1)} all-gather(bf16[1,192,20]{1,2,0:T(8,128)(2,1)S(1)} %bitcast.337), channel_id=1, replica_groups=mesh['expert'=4,'shard'=8] {'shard'}, dimensions={0}, use_global_device_ids=true | all-gather | bytes 69120 | tf_op jit(solution)/shard_map/all_gather | solution.py:121
  192.6 72.3 %all-gather.19.cloned.1.call-done = bf16[1536,1536]{1,0:T(8,128)(2,1)} async-done(((bf16[192,1536]{1,0:T(8,128)(2,1)}), bf16[1536,1536]{1,0:T(8,128)(2,1)}) %all-gather.19.cloned.1.call-update) | async-done | bytes 4718608 | tf_op jit(solution)/shard_map/all_gather | solution.py:116
  272.1 94.1 %while.28 = (s32[]{:T(128)}, bf16[8,384,3,64]{1,3,2,0:T(8,128)(2,1)}, f32[8,3,384]{2,1,0:T(4,128)}, bf16[8,1536,64]{1,2,0:T(8,128)(2,1)}, bf16[8,1536,64]{1,2,0:...) while((s32[]{:T(128)}, ...), condition=%wide.region_4.5_spmd.clone, body=%wide.region_1.4_spmd.clone.sunk | while | flops 479599488 | bytes 24343584 | solution.py:191
  382.7 25.1 %gather_fusion = bf16[5120,1536]{1,0:T(8,128)(2,1)} fusion(bf16[384,1536]{1,0:T(8,128)(2,1)S(1)} %multiply_convert_fusion.3, s32[5120]{0:T(1024)} %get-tuple-element.300), kind=kCustom, calls=%fused_computation | custom fusion | bytes 31477760 | tf_op jit(solution)/shard_map/gather | solution.py:213
  407.9 36.3 %gather_fusion.2 = bf16[5120,1536]{1,0:T(8,128)(2,1)} fusion(bf16[3072,1536]{1,0:T(8,128)(2,1)} %fusion.65, s32[5120]{0:T(1024)S(1)} %copy-done.52), kind=kCustom, calls=%fused_computation.2 | custom fusion | bytes 31477760 | tf_op jit(solution)/shard_map/gather | solution.py:242
  444.1 21.9 broadcast_select_fusion
  473.6 171.1 %all-to-all-done = bf16[4,5,256,1536]{3,2,1,0:T(8,128)(2,1)} async-done(((bf16[4,5,256,1536]{3,2,1,0:T(8,128)(2,1)}), bf16[4,5,256,1536]{3,2,1,0:T(8,128)(2,1)}, u32[]{:S(2)}, u32[]{:S(2)}) %all-to-all-start) | async-done | bytes 15728672 | tf_op jit(solution)/shard_map/all_to_all | solution.py:214
  651.5 16.3 fusion.70
  667.8 16.3 fusion.72
  699.9 123.4 %all-to-all-done.2 = bf16[4,5,256,1536]{3,2,1,0:T(8,128)(2,1)} async-done(((bf16[4,5,256,1536]{3,2,1,0:T(8,128)(2,1)}), bf16[4,5,256,1536]{3,2,1,0:T(8,128)(2,1)}, u32[]{:S(2)}, u32[]{:S(2)}) %all-to-all-start.2) | async-done | bytes 15728672 | tf_op jit(solution)/shard_map/all_to_all | solution.py:243
  823.3 22.8 multiply_convert_fusion
  882.1 18.3 fusion.78
  900.4 21.4 fusion.74
  935.2 118.7 %all-to-all-done.1 = bf16[4,5,256,1536]{3,2,1,0:T(8,128)(2,1)} async-done(((bf16[4,5,256,1536]{3,2,1,0:T(8,128)(2,1)}), bf16[4,5,256,1536]{3,2,1,0:T(8,128)(2,1)}, u32[]{:S(2)}, u32[]{:S(2)}) %all-to-all-start.1) | async-done | bytes 15728672 | tf_op jit(solution)/shard_map/all_to_all | solution.py:229
  1060.8 27.0 %gather_fusion.1 = bf16[3072,1536]{1,0:T(8,128)(2,1)} fusion(bf16[5120,1536]{1,0:T(8,128)(2,1)} %bitcast.27, s32[3072]{0:T(1024)S(1)} %broadcast_clamp_fusion), kind=kCustom, calls=%fused_computation.1 | custom fusion | bytes 18886656 | tf_op jit(solution)/shard_map/gather | solution.py:232
  1101.5 131.0 %all-to-all-done.3 = bf16[4,5,256,1536]{3,2,1,0:T(8,128)(2,1)} async-done(((bf16[4,5,256,1536]{3,2,1,0:T(8,128)(2,1)}), bf16[4,5,256,1536]{3,2,1,0:T(8,128)(2,1)}, u32[]{:S(2)}, u32[]{:S(2)}) %all-to-all-start.3) | async-done | bytes 15728672 | tf_op jit(solution)/shard_map/all_to_all | solution.py:268
  1232.5 27.0 %gather_fusion.3 = bf16[3072,1536]{1,0:T(8,128)(2,1)} fusion(bf16[5120,1536]{1,0:T(8,128)(2,1)} %bitcast.36, s32[3072]{0:T(1024)S(1)} %broadcast_clamp_fusion), kind=kCustom, calls=%fused_computation.3 | custom fusion | bytes 18886656 | tf_op jit(solution)/shard_map/gather | solution.py:272
  1280.6 153.1 %while.29 = (s32[]{:T(128)}, f32[8,384,3,64]{1,3,2,0:T(8,128)}, f32[8,1536,64]{1,2,0:T(8,128)}, f32[8,1536,64]{1,2,0:T(8,128)}, bf16[8,1536,64]{1,2,0:T(8,128)(2...) while((s32[]{:T(128)}, f32[8,384,3,64]{1,3,2,0:T(8,128)}, ...), condition=%wide.region_22.23_spmd.clone, body=%wide.region_20.22_spmd.clone.sunk | while | flops 1153866624 | bytes 80168072 | solution.py:294
  1453.0 47.4 %reduce-scatter.31.cloned.1.call-done = bf16[128,512]{1,0:T(8,128)(2,1)} async-done(((bf16[1024,512]{1,0:T(8,128)(2,1)}), bf16[128,512]{1,0:T(8,128)(2,1)}) %reduce-scatter.31.cloned.1.call-update) | async-done | bytes 131088
  1512.9 54.6 %reduce-scatter.33.cloned.1.call-done = bf16[128,512]{1,0:T(8,128)(2,1)} async-done(((bf16[1024,512]{1,0:T(8,128)(2,1)}), bf16[128,512]{1,0:T(8,128)(2,1)}) %reduce-scatter.33.cloned.1.call-update) | async-done | bytes 131088
  1647.8 53.1 %reduce-scatter.19.cloned.1.call-done = bf16[192,512]{1,0:T(8,128)(2,1)} async-done(((bf16[1536,512]{1,0:T(8,128)(2,1)}), bf16[192,512]{1,0:T(8,128)(2,1)}) %reduce-scatter.19.cloned.1.call-update) | async-done | bytes 196624 | tf_op jit(solution)/shard_map/reduce_scatter | solution.py:356
  1700.9 68.3 %reduce-scatter.21.cloned.1.call-done = bf16[192,512]{1,0:T(8,128)(2,1)} async-done(((bf16[1536,512]{1,0:T(8,128)(2,1)}), bf16[192,512]{1,0:T(8,128)(2,1)}) %reduce-scatter.21.cloned.1.call-update) | async-done | bytes 196624 | tf_op jit(solution)/shard_map/reduce_scatter | solution.py:359
  1769.2 98.0 %reduce-scatter.23.cloned.1.call-done = bf16[192,1536]{1,0:T(8,128)(2,1)} async-done(((bf16[1536,1536]{1,0:T(8,128)(2,1)}), bf16[192,1536]{1,0:T(8,128)(2,1)}) %reduce-scatter.23.cloned.1.call-update) | async-done | bytes 589840 | tf_op jit(solution)/shard_map/reduce_scatter | solution.py:362
  1867.2 98.9 %reduce-scatter.17.cloned.1.call-done = bf16[192,1536]{1,0:T(8,128)(2,1)} async-done(((bf16[1536,1536]{1,0:T(8,128)(2,1)}), bf16[192,1536]{1,0:T(8,128)(2,1)}) %reduce-scatter.17.cloned.1.call-update) | async-done | bytes 589840 | tf_op jit(solution)/shard_map/reduce_scatter | solution.py:353
  1967.4 21.9 all-reduce.4
  2010.6 99.1 %reduce-scatter.29.cloned.1.call-done = bf16[5,64,1536]{2,1,0:T(8,128)(2,1)} async-done(((bf16[5,512,1536]{2,1,0:T(8,128)(2,1)}), bf16[5,64,1536]{2,1,0:T(8,128)(2,1)}) %reduce-scatter.29.cloned.1.call-update) | async-done | bytes 983056 | tf_op jit(solution)/shard_map/reduce_scatter | solution.py:377
  2112.3 140.1 %reduce-scatter.27.cloned.1.call-done = bf16[5,192,512]{2,1,0:T(8,128)(2,1)} async-done(((bf16[5,1536,512]{2,1,0:T(8,128)(2,1)}), bf16[5,192,512]{2,1,0:T(8,128)(2,1)}) %reduce-scatter.27.cloned.1.call-update) | async-done | bytes 983056 | tf_op jit(solution)/shard_map/reduce_scatter | solution.py:374
  2255.2 140.2 %reduce-scatter.25.cloned.1.call-done = bf16[5,192,512]{2,1,0:T(8,128)(2,1)} async-done(((bf16[5,1536,512]{2,1,0:T(8,128)(2,1)}), bf16[5,192,512]{2,1,0:T(8,128)(2,1)}) %reduce-scatter.25.cloned.1.call-update) | async-done | bytes 983056 | tf_op jit(solution)/shard_map/reduce_scatter | solution.py:371
  2398.1 41.7 %all-reduce.10.cloned.1.call-done = (bf16[192,1536]{1,0:T(8,128)(2,1)}, bf16[192,512]{1,0:T(8,128)(2,1)}, bf16[192,512]{1,0:T(8,128)(2,1)}, bf16[192,1536]{1,0:T(8,128)(2,1)}) async-done(((bf16[192,1536]{1,0:T(8,128)(2,1)}, bf16[192,512]{1,0:T(8,128)(2,1)}, bf16[192,512]{1,0:T(8,128)(2,1)}, bf16[192,1536]{1,0:T(8,128)(2,1)}), (bf16[192,1536]{1,0:T(8,128)(2,1)}, bf16[192,512]{1,0:T(8,128)(2,1)}, ...) | async-done | bytes 1572880 | tf_op jit(solution)/shard_map/psum | solution.py:383
  (490 shorter events, 609.1 us)
Async XLA Ops:
  7.2 50.2 %all-gather.11.cloned.1.call-start = ((), (), s32[]{:S(2)}) async-start(), calls=%async_computation.14 | async-start | bytes 1769472 | tf_op jit(solution)/shard_map/all_gather | solution.py:118
  7.9 94.2 %all-gather.15.cloned.1.call-start = ((), (), s32[]{:S(2)}) async-start(), calls=%async_computation.16 | async-start | bytes 1769472 | tf_op jit(solution)/shard_map/all_gather | solution.py:117
  8.7 174.7 %all-gather.13.cloned.1.call-start = ((), (), s32[]{:S(2)}) async-start(), calls=%async_computation.15 | async-start | bytes 1179648 | tf_op jit(solution)/shard_map/all_gather | solution.py:179
  60.7 129.3 %all-gather.17.cloned.1.call-start = ((), (), s32[]{:S(2)}) async-start(), calls=%async_computation.17 | async-start | bytes 1179648 | tf_op jit(solution)/shard_map/all_gather | solution.py:178
  106.4 158.6 %all-gather.19.cloned.1.call-start = ((), (), s32[]{:S(2)}) async-start(), calls=%async_computation.18 | async-start | bytes 5308416 | tf_op jit(solution)/shard_map/all_gather | solution.py:116
  107.0 259.3 %all-gather.21.cloned.1.call-start = ((), (), s32[]{:S(2)}) async-start(), calls=%async_computation.19 | async-start | bytes 5308416 | tf_op jit(solution)/shard_map/all_gather | solution.py:119
  107.5 544.0 %all-gather.25.cloned.1.call-start = ((), (), s32[]{:S(2)}) async-start(), calls=%async_computation.21 | async-start | bytes 8847360 | tf_op jit(solution)/shard_map/all_gather | solution.py:123
  108.3 559.5 %all-gather.23.cloned.1.call-start = ((), (), s32[]{:S(2)}) async-start(), calls=%async_computation.20 | async-start | bytes 8847360 | tf_op jit(solution)/shard_map/all_gather | solution.py:122
  119.6 63.8 %collective-permute-start = (bf16[256,512]{1,0:T(8,128)(2,1)}, bf16[256,512]{1,0:T(8,128)(2,1)}, u32[]{:S(2)}, u32[]{:S(2)}) collective-permute-start(bf16[256,512]{1,0:T(8,128)(2,1)} %slice.115), channel_id=1, source_target_pairs={{0,1},{1,0},{2,3},{3,2},{4,5},{5,4},{6,7},{7,6},{8,9},{9,8},{10,11... | collective-permute-start | bytes 786440 | tf_op jit(solution)/shard_map/ppermute | solution.py:21
  180.7 196.4 %copy-start.5 = (f32[384,1536]{1,0:T(8,128)}, f32[384,1536]{1,0:T(8,128)S(1)}, u32[]{:S(2)}) copy-start(f32[384,1536]{1,0:T(8,128)S(1)} %convert_element_type.238) | copy-start | bytes 7077892
  183.3 6.7 collective-permute-start.1
  466.0 178.6 %all-to-all-start = ((bf16[4,5,256,1536]{3,2,1,0:T(8,128)(2,1)}), bf16[4,5,256,1536]{3,2,1,0:T(8,128)(2,1)}, u32[]{:S(2)}, u32[]{:S(2)}) async-start(bf16[4,5,256,1536]{3,2,1,0:T(8,128)(2,1)} %get-tuple-element.302), calls=%async_computation | async-start | bytes 31457280 | tf_op jit(solution)/shard_map/all_to_all | solution.py:214
  472.9 227.0 %all-gather.27.cloned.1.call-start = ((), (), s32[]{:S(2)}) async-start(), calls=%async_computation.22 | async-start | bytes 8847360 | tf_op jit(solution)/shard_map/all_gather | solution.py:124
  644.7 178.6 %all-to-all-start.2 = ((bf16[4,5,256,1536]{3,2,1,0:T(8,128)(2,1)}), bf16[4,5,256,1536]{3,2,1,0:T(8,128)(2,1)}, u32[]{:S(2)}, u32[]{:S(2)}) async-start(bf16[4,5,256,1536]{3,2,1,0:T(8,128)(2,1)} %get-tuple-element.301), calls=%async_computation.2 | async-start | bytes 31457280 | tf_op jit(solution)/shard_map/all_to_all | solution.py:243
  874.9 179.0 %all-to-all-start.1 = ((bf16[4,5,256,1536]{3,2,1,0:T(8,128)(2,1)}), bf16[4,5,256,1536]{3,2,1,0:T(8,128)(2,1)}, u32[]{:S(2)}, u32[]{:S(2)}) async-start(bf16[4,5,256,1536]{3,2,1,0:T(8,128)(2,1)} %copy.128), calls=%async_computation.1 | async-start | bytes 31457280 | tf_op jit(solution)/shard_map/all_to_all | solution.py:229
  935.2 125.6 %copy-start.60 = (s32[3072,1]{0,1:T(1,128)S(1)}, s32[3072,1]{0,1:T(1,128)}, u32[]{:S(2)}) copy-start(s32[3072,1]{0,1:T(1,128)} %copy-done.59) | copy-start | bytes 36868
  1053.9 178.6 %all-to-all-start.3 = ((bf16[4,5,256,1536]{3,2,1,0:T(8,128)(2,1)}), bf16[4,5,256,1536]{3,2,1,0:T(8,128)(2,1)}, u32[]{:S(2)}, u32[]{:S(2)}) async-start(bf16[4,5,256,1536]{3,2,1,0:T(8,128)(2,1)} %copy.133), calls=%async_computation.3 | async-start | bytes 31457280 | tf_op jit(solution)/shard_map/all_to_all | solution.py:268
  1060.7 439.6 %reduce-scatter.31.cloned.1.call-start = ((), (), s32[]{:S(2)}) async-start(), calls=%async_computation.30 | async-start | bytes 1179648
  1438.4 129.0 %reduce-scatter.33.cloned.1.call-start = ((), (), s32[]{:S(2)}) async-start(), calls=%async_computation.31 | async-start | bytes 1179648
  1444.1 196.4 %reduce-scatter.35.cloned.1.call-start = ((), (), s32[]{:S(2)}) async-start(), calls=%async_computation.32 | async-start | bytes 442368
  1445.1 7.8 collective-permute-start.2
  1448.2 252.7 %reduce-scatter.19.cloned.1.call-start = ((), (), s32[]{:S(2)}) async-start(), calls=%async_computation.24 | async-start | bytes 1769472 | tf_op jit(solution)/shard_map/reduce_scatter | solution.py:356
  1505.6 263.6 %reduce-scatter.21.cloned.1.call-start = ((), (), s32[]{:S(2)}) async-start(), calls=%async_computation.25 | async-start | bytes 1769472 | tf_op jit(solution)/shard_map/reduce_scatter | solution.py:359
  1505.7 6.4 collective-permute-start.3
  1572.6 294.6 %reduce-scatter.23.cloned.1.call-start = ((), (), s32[]{:S(2)}) async-start(), calls=%async_computation.26 | async-start | bytes 5308416 | tf_op jit(solution)/shard_map/reduce_scatter | solution.py:362
  1578.3 387.8 %reduce-scatter.17.cloned.1.call-start = ((), (), s32[]{:S(2)}) async-start(), calls=%async_computation.23 | async-start | bytes 5308416 | tf_op jit(solution)/shard_map/reduce_scatter | solution.py:353
  1588.4 521.3 %reduce-scatter.29.cloned.1.call-start = ((), (), s32[]{:S(2)}) async-start(), calls=%async_computation.29 | async-start | bytes 8847360 | tf_op jit(solution)/shard_map/reduce_scatter | solution.py:377
  1604.0 648.5 %reduce-scatter.27.cloned.1.call-start = ((), (), s32[]{:S(2)}) async-start(), calls=%async_computation.28 | async-start | bytes 8847360 | tf_op jit(solution)/shard_map/reduce_scatter | solution.py:374
  1619.6 775.8 %reduce-scatter.25.cloned.1.call-start = ((), (), s32[]{:S(2)}) async-start(), calls=%async_computation.27 | async-start | bytes 8847360 | tf_op jit(solution)/shard_map/reduce_scatter | solution.py:371
  1635.1 804.7 %all-reduce.10.cloned.1.call-start = ((), (), s32[]{:S(2)}) async-start(), calls=%async_computation.33 | async-start | bytes 3145728 | tf_op jit(solution)/shard_map/psum | solution.py:383
  1644.5 322.8 %copy-start.68 = (bf16[1536]{0:T(1024)(128)(2,1)S(1)}, bf16[1536]{0:T(1024)(128)(2,1)}, u32[]{:S(2)}) copy-start(bf16[1536]{0:T(1024)(128)(2,1)} %get-tuple-element.199) | copy-start | bytes 9220
  1644.5 362.6 %copy-start.13 = (f32[384,1536]{1,0:T(8,128)S(1)}, f32[384,1536]{1,0:T(8,128)}, u32[]{:S(2)}) copy-start(f32[384,1536]{1,0:T(8,128)} %copy-done.11) | copy-start | bytes 7077892
  (89 other events, 802.8 us)
Sparse Core Ops, SparseCore 0:
  10.2 47.1 all-gather.10
  59.6 42.5 all-gather.14
  104.8 39.1 all-gather.12
  146.5 38.2 all-gather.16
  186.8 78.0 all-gather.18
  267.0 77.6 all-gather.20
  346.9 116.2 all-gather.24
  465.4 116.0 all-gather.22
  583.8 116.0 all-gather.26
  1438.6 61.7 reduce-scatter.30
  1504.4 63.0 reduce-scatter.32
  1571.1 61.1 reduce-scatter.34
  1636.3 64.5 reduce-scatter.18
  1704.8 64.3 reduce-scatter.20
  1772.7 94.4 reduce-scatter.22
  1870.7 95.3 reduce-scatter.16
  1969.5 140.0 reduce-scatter.28
  2113.1 139.2 reduce-scatter.26
  2256.1 139.2 reduce-scatter.24
  2397.8 41.9 all-reduce.9
where the time goes:
time: 2470 us; the launch traced here: 2450 us
  waiting for transfers between devices  1550 us (63%)
  matrix products  365 us (15%)
  local copies, waits for them, and re-layouts  215 us (9%)
  other arithmetic  187 us (8%)
  blocking collectives  88.2 us (4%)
  starting transfers between devices  31.6 us (1%)
    all_to_all x1, waiting for transfers between devices, body(): lax.all_to_all(outgoing.reshape(groups, experts_here, capacity, model_wid...  171 us
    reduce_scatter x1, waiting for transfers between devices, body(): lax.psum_scatter(term_gate.astype(jnp.bfloat16), 'shard', scatter_dimensi...  140 us
    reduce_scatter x1, waiting for transfers between devices, body(): lax.psum_scatter(term_up.astype(jnp.bfloat16), 'shard', scatter_dimension...  140 us
    all_to_all x1, waiting for transfers between devices, body(): lax.all_to_all(grad_rows, 'expert', split_axis=0, concat_axis=0, tiled=True)  131 us
    all_to_all x1, waiting for transfers between devices, body(): lax.all_to_all(grad_slots.reshape(groups, experts_here, capacity, model_w...  123 us
    all_to_all x1, waiting for transfers between devices, body(): lax.all_to_all(expert_out, 'expert', split_axis=0, concat_axis=0, tiled=T...  119 us
    unnamed x23, waiting for transfers between devices  107 us
    reduce_scatter x1, waiting for transfers between devices, body(): lax.psum_scatter(term_down.astype(jnp.bfloat16), 'shard', scatter_dimensi...  99.1 us
  transfers between devices with their start and end apart: 28, of which 21 were waited for; matrix products, arithmetic and copies ran while one was open for 20% of the time, Pallas kernels for 0%

commit v1 on v0

v1 whole, which is shorter than its diff:
```python
import functools

import jax
import jax.numpy as jnp
from jax import lax
from jax.experimental import pallas as pl
from jax.experimental.pallas import tpu as pltpu
from jax.sharding import Mesh
from jax.sharding import PartitionSpec as P

HS = 64
PR_DEV = 128

epsilon = 1e-05
negative = -1e30
bf16 = jnp.bfloat16
f32 = jnp.float32
EXPERT = ("y", "c")
SHARD = ("z", "x")


def other(block, axis):
    return lax.ppermute(block, axis, [(0, 1), (1, 0)])


def pick(flag, when_one, when_zero):
    return jnp.where(flag == 1, when_one, when_zero)


def all_pairs():
    return all(lax.axis_size(axis) == 2 for axis in ("y", "c", "x"))


def gather_experts(block):
    if not all_pairs():
        return lax.all_gather(block, EXPERT, axis=0)
    pair = jnp.stack([block, other(block, "y")])
    return jnp.concatenate([pair, other(pair, "c")], 0)


def spread_experts(blocks):
    if not all_pairs():
        return lax.all_to_all(blocks, EXPERT, split_axis=0, concat_axis=0, tiled=True)
    here = lax.axis_index(EXPERT)

    def at(apart):
        return lax.dynamic_index_in_dim(blocks, here ^ apart, 0, keepdims=False)

    across = other(jnp.stack([at(2), at(3)]), "y")
    far = other(jnp.stack([at(1), across[1]]), "c")
    return jnp.stack([at(0), across[0], far[0], far[1]])


def absolute_order(stacked):
    count = stacked.shape[0]
    if not all_pairs():
        return [stacked[place] for place in range(count)]
    here = lax.axis_index(EXPERT)
    slot_of = [0, 2, 1, 3]
    table = jnp.array(slot_of, jnp.int32)
    return [
        lax.dynamic_index_in_dim(stacked, table[here ^ place], 0, keepdims=False)
        for place in range(count)
    ]


def gather_tokens(block):
    if not all_pairs():
        return lax.all_gather(block, EXPERT + ("x",), axis=0, tiled=True)
    half = block.shape[0] // 2
    from_x, from_y = other(block, "x"), other(block, "y")
    near = [block, from_x, from_y, other(from_x[:half], "y"), other(from_y[half:], "x")]
    return jnp.concatenate(near + [other(piece, "c") for piece in near], 0)


def reduce_tokens(partial, count):
    if not all_pairs():
        return lax.psum_scatter(
            partial(0, count), EXPERT + ("x",), scatter_dimension=0, tiled=True
        ).astype(f32)
    rows = count // 8
    far = other(partial(4 * rows, count), "c")
    near = partial(0, 4 * rows)
    half = rows // 2

    def piece(place, start):
        part = slice(place * rows + start, place * rows + start + half)
        return near[part].astype(f32) + far[part].astype(f32)

    def sent(value, axis):
        return other(value.astype(bf16), axis).astype(f32)

    across_x, across_y = sent(piece(3, 0), "x"), sent(piece(3, half), "y")
    own_x, own_y = sent(piece(1, 0), "x"), sent(piece(2, half), "y")
    first = piece(0, 0) + own_x + sent(piece(2, 0) + across_x, "y")
    second = piece(0, half) + own_y + sent(piece(1, half) + across_y, "x")
    return jnp.concatenate([first, second], 0)


def rotated(values):
    width = values.shape[-1]
    lane = lax.broadcasted_iota(jnp.int32, values.shape, values.ndim - 1)
    low = lane % HS < HS // 2
    return jnp.where(
        low, -jnp.roll(values, -(HS // 2), -1), jnp.roll(values, HS // 2, -1)
    )


def rope_tables(positions, width):
    inv_freq = 10000.0 ** (-jnp.arange(HS // 2, dtype=f32) * 2.0 / HS)
    inv_freq = jnp.tile(inv_freq, width // (HS // 2))
    angles = positions.astype(f32)[:, None] * inv_freq[None, :]
    return jnp.cos(angles), jnp.sin(angles)


def norm_rows(values, gain_row):
    inverse = lax.rsqrt(jnp.mean(values * values, -1, keepdims=True) + epsilon)
    normed = values * inverse
    return normed, inverse, normed * gain_row


def norm_back(grad_out, normed, inverse, gain_row):
    scaled = grad_out * gain_row
    grad_in = inverse * (scaled - normed * jnp.mean(scaled * normed, -1, keepdims=True))
    return grad_in, jnp.sum(grad_out * normed, 0)


def nt(left, right):
    return lax.dot_general(left, right, (((1,), (1,)), ((), ())), preferred_element_type=f32)


def nn(left, right):
    return jnp.dot(left, right, preferred_element_type=f32)


def tn(left, right):
    return lax.dot_general(left, right, (((0,), (0,)), ((), ())), preferred_element_type=f32)


def masked_scores(place, keys, query, rows, first_row, prompt_len, half_len):
    if first_row == 0:
        scores = nt(keys[:prompt_len], query)
        key = lax.broadcasted_iota(jnp.int32, scores.shape, 0)
        row = lax.broadcasted_iota(jnp.int32, scores.shape, 1)
        return jnp.where(key - row <= place * PR_DEV, scores, negative)
    ahead = nt(keys[:prompt_len], query)
    scores = nt(keys[prompt_len:], query)
    key = lax.broadcasted_iota(jnp.int32, scores.shape, 0)
    row = lax.broadcasted_iota(jnp.int32, scores.shape, 1)
    limit = jnp.where(key < half_len, row + place % 2 - 1, row + half_len)
    return jnp.concatenate([ahead, jnp.where(key <= limit, scores, negative)], 0)


def attend_kernel(axis_sizes, group, prompt_len, q_ref, kv_ref, out_ref, log_ref):
    place = lax.axis_index("z") * axis_sizes + lax.axis_index("x")
    tok_rows = q_ref.shape[1]
    half_len = tok_rows - PR_DEV
    kv_heads = kv_ref.shape[2] // (2 * HS)
    for kv_head in range(kv_heads):
        keys = kv_ref[0, :, kv_head * HS : (kv_head + 1) * HS]
        values = kv_ref[0, :, (kv_heads + kv_head) * HS : (kv_heads + kv_head + 1) * HS]
        values_t = values.T
        for member in range(group):
            head = kv_head * group + member
            for first, rows in ((0, PR_DEV), (PR_DEV, half_len)):
                query = q_ref[0, first : first + rows, head * HS : (head + 1) * HS]
                scores = masked_scores(place, keys, query, rows, first, prompt_len, half_len)
                row_max = jnp.max(scores, 0, keepdims=True)
                weight = jnp.exp(scores - row_max)
                total = jnp.sum(weight, 0, keepdims=True)
                mixed = nn(values_t[:, : scores.shape[0]], weight.astype(bf16)) / total
                out_ref[0, first : first + rows, head * HS : (head + 1) * HS] = mixed.T.astype(bf16)
                log_ref[0, head : head + 1, first : first + rows] = row_max + jnp.log(total)


def attend_back_kernel(
    axis_sizes, group, prompt_len, q_ref, kv_ref, grad_ref, log_ref, dq_ref, dkv_ref
):
    place = lax.axis_index("z") * axis_sizes + lax.axis_index("x")
    tok_rows = q_ref.shape[1]
    half_len = tok_rows - PR_DEV
    kv_heads = kv_ref.shape[2] // (2 * HS)
    for kv_head in range(kv_heads):
        key_cols = slice(kv_head * HS, (kv_head + 1) * HS)
        value_cols = slice((kv_heads + kv_head) * HS, (kv_heads + kv_head + 1) * HS)
        keys = kv_ref[0, :, key_cols]
        values = kv_ref[0, :, value_cols]
        keys_t = keys.T
        grad_keys = [0.0, 0.0]
        grad_values = [0.0, 0.0]
        for member in range(group):
            head = kv_head * group + member
            for part, (first, rows) in enumerate(((0, PR_DEV), (PR_DEV, half_len))):
                cols = slice(head * HS, (head + 1) * HS)
                query = q_ref[0, first : first + rows, cols]
                grad = grad_ref[0, first : first + rows, cols]
                scores = masked_scores(place, keys, query, rows, first, prompt_len, half_len)
                probs = jnp.exp(scores - log_ref[0, head : head + 1, first : first + rows])
                count = scores.shape[0]
                grad_probs = nt(values[:count], grad)
                delta = jnp.sum(probs * grad_probs, 0, keepdims=True)
                grad_scores = (probs * (grad_probs - delta)).astype(bf16)
                grad_values[part] += nn(probs.astype(bf16), grad)
                grad_keys[part] += nn(grad_scores, query)
                dq = nn(keys_t[:, :count], grad_scores) * HS ** (-0.5)
                dq_ref[0, first : first + rows, cols] = dq.T
        for cols, parts in ((key_cols, grad_keys), (value_cols, grad_values)):
            dkv_ref[0, :prompt_len, cols] = (parts[0] + parts[1][:prompt_len]).astype(bf16)
            dkv_ref[0, prompt_len:, cols] = parts[1][prompt_len:].astype(bf16)


def whole_block(shape):
    return pl.BlockSpec((1,) + shape[1:], lambda step: (step, 0, 0))


def attend(queries, all_kv, group, prompt_len):
    count, tok_rows, width = queries.shape
    keys = all_kv.shape[1]
    heads = count * width // HS
    log_shape = (count, width // HS, tok_rows)
    return pl.pallas_call(
        functools.partial(attend_kernel, lax.axis_size("x"), group, prompt_len),
        grid=(count,),
        in_specs=[whole_block(queries.shape), whole_block(all_kv.shape)],
        out_specs=[whole_block(queries.shape), whole_block(log_shape)],
        out_shape=[
            jax.ShapeDtypeStruct(queries.shape, bf16),
            jax.ShapeDtypeStruct(log_shape, f32),
        ],
        cost_estimate=pl.CostEstimate(
            flops=16 * heads * tok_rows * keys * HS,
            transcendentals=heads * tok_rows * keys,
            bytes_accessed=8 * queries.size + 2 * all_kv.size,
        ),
        compiler_params=pltpu.CompilerParams(vmem_limit_bytes=48 << 20),
        name="attend",
    )(queries, all_kv)


def attend_back(queries, all_kv, grads, logs, group, prompt_len):
    count, tok_rows, width = queries.shape
    keys = all_kv.shape[1]
    heads = count * width // HS
    return pl.pallas_call(
        functools.partial(attend_back_kernel, lax.axis_size("x"), group, prompt_len),
        grid=(count,),
        in_specs=[whole_block(value.shape) for value in (queries, all_kv, grads, logs)],
        out_specs=[whole_block(queries.shape), whole_block(all_kv.shape)],
        out_shape=[
            jax.ShapeDtypeStruct(queries.shape, f32),
            jax.ShapeDtypeStruct(all_kv.shape, bf16),
        ],
        cost_estimate=pl.CostEstimate(
            flops=40 * heads * tok_rows * keys * HS,
            transcendentals=heads * tok_rows * keys,
            bytes_accessed=12 * queries.size + 6 * all_kv.size,
        ),
        compiler_params=pltpu.CompilerParams(vmem_limit_bytes=56 << 20),
        name="attend_back",
    )(queries, all_kv, grads, logs)


def body(
    hidden_in,
    cotangent,
    routes,
    attn_gain,
    q_weight,
    k_weight,
    v_weight,
    o_weight,
    ffn_gain,
    router_weight,
    gate_weight,
    up_weight,
    down_weight,
):
    tok_rows, model_width = hidden_in.shape
    odd = lax.axis_index("x")
    shard_pos = lax.axis_index(SHARD)
    expert_pos = lax.axis_index(EXPERT)
    expert_size = lax.axis_size(EXPERT)
    shards = lax.axis_size(SHARD)
    pairs = lax.axis_size("z")
    experts_here, shard_rows, inner_width = gate_weight.shape
    experts_all = router_weight.shape[1]
    piece = inner_width // shards
    half_width = inner_width // 2
    half_len = tok_rows - PR_DEV
    prompt_len = PR_DEV * shards
    q_cols = q_weight.shape[1] // expert_size
    k_cols = k_weight.shape[1] // expert_size
    o_cols = o_weight.shape[1] // expert_size
    group = q_weight.shape[1] // k_weight.shape[1]
    qkv_cols = q_cols + 2 * k_cols

    def columns_here(weight):
        width = weight.shape[1] // expert_size
        return lax.dynamic_slice_in_dim(weight, expert_pos * width, width, 1)

    small = jnp.concatenate(
        [
            attn_gain[:, None],
            ffn_gain[:, None],
            router_weight,
            jnp.zeros((shard_rows, 126 - experts_all), bf16),
        ],
        1,
    )
    first_shard = jnp.concatenate(
        [
            columns_here(q_weight),
            columns_here(k_weight),
            columns_here(v_weight),
            columns_here(o_weight),
            small,
        ],
        1,
    )
    everyone = EXPERT + SHARD
    first_all = lax.all_gather(first_shard, everyone, axis=0, tiled=True)
    first_all = first_all.reshape(expert_size, model_width, qkv_cols + o_cols + 128)
    w_qkv = first_all[:, :, :qkv_cols]
    w_out = first_all[:, :, qkv_cols : qkv_cols + o_cols]
    small_all = first_all[0, :, qkv_cols + o_cols :]
    gain_one = small_all[:, 0].astype(f32)
    gain_two = small_all[:, 1].astype(f32)
    w_router = small_all[:, 2 : 2 + experts_all]

    def halves(weight):
        cut = weight.reshape(experts_here, shard_rows, pairs, 2, piece)
        cut = cut.transpose(3, 1, 2, 0, 4).reshape(2, shard_rows, experts_here * half_width)
        return cut

    both = jnp.concatenate([halves(gate_weight), halves(up_weight)], 2)
    kept, given = pick(odd, both[1], both[0]), pick(odd, both[0], both[1])
    received = other(given, "x")
    mine = jnp.concatenate([pick(odd, received, kept), pick(odd, kept, received)], 0)
    w_gate_up = lax.all_gather(mine, "z", axis=0, tiled=True)
    w_down = lax.all_gather(
        down_weight.reshape(experts_here * piece, model_width), "z", axis=0, tiled=True
    )
    cot_all = gather_tokens(cotangent)

    row_index = jnp.arange(tok_rows, dtype=jnp.int32)
    positions = jnp.where(
        row_index < PR_DEV,
        shard_pos * PR_DEV + row_index,
        prompt_len + 2 * (row_index - PR_DEV) + odd,
    )
    q_cos, q_sin = rope_tables(positions, q_cols)
    k_cos, k_sin = q_cos[:, :k_cols], q_sin[:, :k_cols]
    x_float = hidden_in.astype(f32)
    normed_one, inverse_one, scaled_one = norm_rows(x_float, gain_one)
    attn_input = scaled_one.astype(bf16)
    lin = jnp.einsum("td,qdc->qtc", attn_input, w_qkv, preferred_element_type=f32)
    q_lin, k_lin, v_lin = (
        lin[:, :, :q_cols],
        lin[:, :, q_cols : q_cols + k_cols],
        lin[:, :, q_cols + k_cols :],
    )
    queries = (q_lin * q_cos + rotated(q_lin) * q_sin).astype(bf16) * bf16(HS ** (-0.5))
    keys = (k_lin * k_cos + rotated(k_lin) * k_sin).astype(bf16)
    kv = jnp.concatenate([keys, v_lin.astype(bf16)], 2)
    kv_flat = kv.transpose(1, 0, 2).reshape(tok_rows, expert_size * 2 * k_cols)
    prompt_kv = lax.all_gather(kv_flat[:PR_DEV], SHARD, axis=0, tiled=True)
    partner_kv = other(kv_flat[PR_DEV:], "x")
    all_kv = jnp.concatenate([prompt_kv, partner_kv, kv_flat[PR_DEV:]], 0)
    all_kv = all_kv.reshape(-1, expert_size, 2 * k_cols).transpose(1, 0, 2)
    mix_blocks, logs = attend(queries, all_kv, group, prompt_len)
    attn_mix = mix_blocks.transpose(1, 0, 2).reshape(tok_rows, -1)
    branch = jnp.concatenate([nn(attn_mix, w_out[place]) for place in range(expert_size)], 1)
    residual = x_float + branch
    normed_two, inverse_two, scaled_two = norm_rows(residual, gain_two)
    ffn_input = scaled_two.astype(bf16)

    logits = nn(ffn_input, w_router)
    expert_ids = jnp.arange(experts_all, dtype=jnp.int32)
    taken = jnp.any(routes[:, :, None] == expert_ids[None, None, :], 1)
    masked = jnp.where(taken, logits, negative)
    raised = jnp.where(taken, jnp.exp(masked - jnp.max(masked, -1, keepdims=True)), 0.0)
    gates = raised / jnp.sum(raised, -1, keepdims=True)
    gates_high = gates.astype(bf16)
    gates_low = (gates - gates_high.astype(f32)).astype(bf16)
    lanes = jnp.arange(128, dtype=jnp.int32)[None, :]
    placed = nn(gates_high, (lanes == expert_ids[:, None]).astype(bf16)) + nn(
        gates_low, (lanes == experts_all + expert_ids[:, None]).astype(bf16)
    )
    sent = jnp.concatenate([ffn_input, placed.astype(bf16)], 1)
    token_all = gather_tokens(sent)
    rows_all = token_all[:, :model_width]

    width = experts_here * half_width
    column_expert = jnp.arange(width, dtype=jnp.int32) // piece % experts_here
    column_expert = column_expert + expert_pos * experts_here
    source = jnp.arange(128, dtype=jnp.int32)[:, None]
    to_columns = (source == column_expert[None, :]) | (
        source == experts_all + column_expert[None, :]
    )
    spread = nn(token_all[:, model_width:], to_columns.astype(bf16))
    gate_up = nn(rows_all, w_gate_up)
    gate_proj, up_proj = gate_up[:, :width], gate_up[:, width:]
    sig_gate = jax.nn.sigmoid(gate_proj)
    silu_gate = gate_proj * sig_gate
    inner_act = (silu_gate * up_proj).astype(bf16).astype(f32)
    gated = (inner_act * spread).astype(bf16)
    term_down = tn(gated, cot_all).astype(bf16)
    w_down, term_down = lax.optimization_barrier((w_down, term_down))
    grad_plain = nt(cot_all, w_down)
    extra = -(-4 * experts_all // 128) * 128
    target = jnp.arange(extra, dtype=jnp.int32)[None, :]
    from_columns = (target == odd * experts_all + column_expert[:, None]) | (
        target == (2 + odd) * experts_all + column_expert[:, None]
    )
    gates_grad = nn((inner_act * grad_plain).astype(bf16), from_columns.astype(bf16))
    grads_high = gates_grad.astype(bf16)
    grads_low = (gates_grad - grads_high.astype(f32)).astype(bf16)
    returned = jnp.where(target < 2 * experts_all, grads_high, grads_low)
    grad_inner = grad_plain * spread
    grad_gate_proj = (
        grad_inner * up_proj * sig_gate * (1.0 + gate_proj * (1.0 - sig_gate))
    ).astype(bf16)
    grad_up_proj = (grad_inner * silu_gate).astype(bf16)
    grad_both = jnp.concatenate([grad_gate_proj, grad_up_proj], 1)

    def back_rows(start, stop):
        rows = nt(grad_both[start:stop], w_gate_up).astype(bf16)
        return jnp.concatenate([rows, returned[start:stop]], 1)

    back = reduce_tokens(back_rows, rows_all.shape[0])
    back, gates_back = back[:, :model_width], back[:, model_width:]
    grad_down = lax.psum_scatter(term_down, "z", scatter_dimension=0, tiled=True)
    grad_down = grad_down.astype(f32).reshape(experts_here, piece, model_width)
    term_gate = tn(rows_all, grad_gate_proj).astype(bf16)
    term_up = tn(rows_all, grad_up_proj).astype(bf16)

    def from_both_halves(term):
        summed = lax.psum_scatter(term, "z", scatter_dimension=0, tiled=True)
        upper, lower = summed[:shard_rows], summed[shard_rows:]
        kept, given = pick(odd, lower, upper), pick(odd, upper, lower)
        received = other(given, "x")
        sides = jnp.stack([pick(odd, received, kept), pick(odd, kept, received)])
        sides = sides.astype(f32).reshape(2, shard_rows, pairs, experts_here, piece)
        return sides.transpose(3, 1, 2, 0, 4).reshape(experts_here, shard_rows, inner_width)

    grad_gate = from_both_halves(term_gate)

    grad_y = cotangent.astype(f32)
    gates_back = sum(
        gates_back[:, part * experts_all : (part + 1) * experts_all] for part in range(4)
    )
    centered = gates_back - jnp.sum(gates_back * gates, -1, keepdims=True)
    grad_logits = (gates * centered).astype(bf16)
    grad_ffn_input = back + nt(grad_logits, w_router)
    term_router = tn(ffn_input, grad_logits)
    grad_resid_norm, term_gain_two = norm_back(grad_ffn_input, normed_two, inverse_two, gain_two)
    grad_residual = grad_y + grad_resid_norm
    grad_branch = grad_residual.astype(bf16)
    branch_blocks = grad_branch.reshape(tok_rows, expert_size, o_cols).transpose(1, 0, 2)
    grad_mix = jnp.einsum("qtd,qcd->tc", branch_blocks, w_out, preferred_element_type=f32)
    grad_mix = grad_mix.astype(bf16).reshape(tok_rows, expert_size, q_cols).transpose(1, 0, 2)

    inputs_all = gather_experts(attn_input).reshape(-1, model_width)
    mixes_all = gather_experts(attn_mix).reshape(-1, model_width)
    grad_mix, term_gate_done, term_up, inputs_all, mixes_all = lax.optimization_barrier(
        (grad_mix, term_gate, term_up, inputs_all, mixes_all)
    )
    grad_queries, grad_kv = attend_back(queries, all_kv, grad_mix, logs, group, prompt_len)
    grad_kv = grad_kv.transpose(1, 0, 2).reshape(-1, expert_size * 2 * k_cols)
    prompt_grad = lax.psum_scatter(
        grad_kv[:prompt_len], SHARD, scatter_dimension=0, tiled=True
    ).astype(f32)
    gated, grad_kv = lax.optimization_barrier((gated, grad_kv))
    mixture = reduce_tokens(
        lambda start, stop: nn(gated[start:stop], w_down).astype(bf16), rows_all.shape[0]
    )
    hidden_out = (residual + mixture).astype(bf16)
    term_up, prompt_grad = lax.optimization_barrier((term_up, prompt_grad))
    grad_up = from_both_halves(term_up)
    partner_grad = other(grad_kv[prompt_len : prompt_len + half_len], "x").astype(f32)
    own_grad = grad_kv[prompt_len + half_len :].astype(f32) + partner_grad
    own_grad = jnp.concatenate([prompt_grad, own_grad], 0)
    own_grad = own_grad.reshape(tok_rows, expert_size, 2 * k_cols).transpose(1, 0, 2)
    grad_keys, grad_values = own_grad[:, :, :k_cols], own_grad[:, :, k_cols:]
    grad_lin = jnp.concatenate(
        [
            grad_queries * q_cos - rotated(grad_queries * q_sin),
            grad_keys * k_cos - rotated(grad_keys * k_sin),
            grad_values,
        ],
        2,
    ).astype(bf16)
    grad_attn_input = jnp.einsum("qtc,qdc->td", grad_lin, w_qkv, preferred_element_type=f32)
    grad_x_norm, term_gain_one = norm_back(grad_attn_input, normed_one, inverse_one, gain_one)
    grad_hidden = (grad_residual + grad_x_norm).astype(bf16)

    lin_all = spread_experts(grad_lin).reshape(-1, qkv_cols)
    branch_all = spread_experts(branch_blocks).reshape(-1, o_cols)
    term_qkv = tn(inputs_all, lin_all)
    term_out = tn(mixes_all, branch_all)
    gains = jnp.concatenate(
        [term_gain_one[None], term_gain_two[None], jnp.zeros((126, model_width), f32)], 0
    )
    shift = (lanes == 2 + expert_ids[:, None]).astype(bf16)
    small_terms = gains.T.astype(bf16) + nn(term_router.astype(bf16), shift).astype(bf16)
    terms = jnp.concatenate([term_qkv.astype(bf16), term_out.astype(bf16), small_terms], 1)
    terms = lax.psum_scatter(terms, SHARD, scatter_dimension=0, tiled=True)
    stacked = gather_experts(terms)
    blocks = [block.astype(f32) for block in absolute_order(stacked)]

    def columns(start, width):
        return jnp.concatenate([block[:, start : start + width] for block in blocks], 1)

    tail = sum(block[:, qkv_cols + o_cols :] for block in blocks)
    return (
        hidden_out,
        grad_hidden,
        tail[:, 0],
        columns(0, q_cols),
        columns(q_cols, k_cols),
        columns(q_cols + k_cols, k_cols),
        columns(qkv_cols, o_cols),
        tail[:, 1],
        tail[:, 2 : 2 + experts_all],
        grad_gate,
        grad_up,
        grad_down,
    )


def solution(mesh):
    devices = mesh.devices
    expert_size, shards = devices.shape
    fine = Mesh(
        devices.reshape(expert_size // 2, 2, shards // 2, 2), EXPERT + SHARD
    )
    rows = P(EXPERT + SHARD, None)
    vector, matrix = P(SHARD), P(SHARD, None)
    experts = P(EXPERT, SHARD, None)
    return jax.shard_map(
        body,
        mesh=fine,
        in_specs=(
            rows,
            rows,
            rows,
            vector,
            matrix,
            matrix,
            matrix,
            matrix,
            vector,
            matrix,
            experts,
            experts,
            experts,
        ),
        out_specs=(
            rows,
            rows,
            vector,
            matrix,
            matrix,
            matrix,
            matrix,
            vector,
            matrix,
            experts,
            experts,
            experts,
        ),
        check_vma=False,
    )
```

time: 2470 us -> 1090 us (0.44)
  waiting for transfers between devices: 1550 us -> 457 us
  matrix products: 365 us -> 245 us
  other arithmetic: 187 us -> 96 us
  blocking collectives: 88.2 us -> 0 us
  Pallas kernels: 0 us -> 73.2 us
  local copies, waits for them, and re-layouts: 215 us -> 149 us
    reduce_scatter x7 -> x4, waiting for transfers between devices: 698 us -> 147 us  [the longest x2 73.2 us: from_both_halves(): summed = lax.psum_scatter(term, 'z', scatter_dimension=0, tiled=True)]
    all_to_all x4 -> x0, waiting for transfers between devices: 544 us -> none  [the longest x1 171 us: body(): lax.all_to_all(outgoing.reshape(groups, experts_here, capacity, model_wid...]
    ppermute x4 -> x47, waiting for transfers between devices: 9.78 us -> 171 us  [other(): return lax.ppermute(block, axis, [(0, 1), (1, 0)])]
    dot_general x80 -> x25, matrix products: 365 us -> 245 us  [the longest x13 98.3 us: nn(): return jnp.dot(left, right, preferred_element_type=f32)]
    gather x4 -> x0, local copies, waits for them, and re-layouts: 115 us -> none  [the longest x1 36.3 us: body(): grad_route[slot_route]]
    pallas_call x0 -> x2, Pallas kernels: none -> 73.2 us  [the longest x1 51.1 us: attend_back(): pl.pallas_call(functools.partial(attend_back_kernel, lax.axis_size('x'),...]
    unnamed x23 -> x10, waiting for transfers between devices: 107 us -> 36.7 us
    select_n x18 -> x6, other arithmetic: 64.4 us -> 11.1 us  [pick(): return jnp.where(flag == 1, when_one, when_zero)]
  transfers between devices with their start and end apart: 28 -> 56, of which waited for: 21 -> 22; matrix products, arithmetic and copies ran while one was open for 20% -> 33% of each run, Pallas kernels for 0% -> 2%
where the time goes in v1:
time: 1090 us; the launch traced here: 1080 us
  waiting for transfers between devices  457 us (42%)
  matrix products  245 us (22%)
  local copies, waits for them, and re-layouts  149 us (14%)
  other arithmetic  96 us (9%)
  Pallas kernels  73.2 us (7%)
  starting transfers between devices  40.2 us (4%)
  between operations  23.6 us (2%)
    ppermute x47, waiting for transfers between devices, other(): return lax.ppermute(block, axis, [(0, 1), (1, 0)])  171 us
    all_gather x1, waiting for transfers between devices, body(): first_all = lax.all_gather(first_shard, everyone, axis=0, tiled=True)  103 us
    dot_general x13, matrix products, nn(): return jnp.dot(left, right, preferred_element_type=f32)  98.3 us
    reduce_scatter x2, waiting for transfers between devices, from_both_halves(): summed = lax.psum_scatter(term, 'z', scatter_dimension=0, tiled=True)  73.2 us
    dot_general x4, matrix products, nt(): lax.dot_general(left, right, (((1,), (1,)), ((), ())), preferred_element_...  69.7 us
    unnamed x241, local copies, waits for them, and re-layouts  65.8 us
    dot_general x5, matrix products, tn(): lax.dot_general(left, right, (((0,), (0,)), ((), ())), preferred_element_...  59.9 us
    reduce_scatter x1, waiting for transfers between devices, body(): terms = lax.psum_scatter(terms, SHARD, scatter_dimension=0, tiled=True)  57.3 us
  transfers between devices with their start and end apart: 56, of which 22 were waited for; matrix products, arithmetic and copies ran while one was open for 33% of the time, Pallas kernels for 2%

profile of v1, /device:TPU:0, one launch (start us, length us, event | category | flops | bytes accessed | tf_op | source)
XLA Modules:
  0.0 1083.8 jit_solution(13664468276262307720)
XLA Ops:
  15.2 102.6 %all-gather.5.cloned.1.call-done = bf16[6144,1152]{1,0:T(8,128)(2,1)} async-done(((bf16[192,1152]{1,0:T(8,128)(2,1)}), bf16[6144,1152]{1,0:T(8,128)(2,1)}) %all-gather.5.cloned.1.call-update) | async-done | bytes 14155792 | tf_op jit(solution)/shard_map/all_gather | solution.py:321
  119.7 6.1 fusion.58
  143.8 31.7 %collective-permute-done.10 = bf16[192,2560]{1,0:T(8,128)(2,1)} collective-permute-done((bf16[192,2560]{1,0:T(8,128)(2,1)}, bf16[192,2560]{1,0:T(8,128)(2,1)}, u32[]{:S(2)}, u32[]{:S(2)}) %collective-permute-start.10) | collective-permute-done | bytes 983072 | tf_op jit(solution)/shard_map/ppermute | solution.py:23
  189.7 19.5 %collective-permute-done.11 = bf16[384,1536]{1,0:T(8,128)(2,1)} collective-permute-done((bf16[384,1536]{1,0:T(8,128)(2,1)}, bf16[384,1536]{1,0:T(8,128)(2,1)}, u32[]{:S(2)}, u32[]{:S(2)}) %collective-permute-start.11) | collective-permute-done | bytes 1179680 | tf_op jit(solution)/shard_map/ppermute | solution.py:23
  247.6 22.2 %attend.1 = (bf16[4,384,384]{2,1,0:T(8,128)(2,1)S(1)}, f32[4,6,384]{2,1,0:T(8,128)S(1)}) custom-call(bf16[4,384,384]{2,1,0:T(8,128)(2,1)S(1)} %fusion.71.q_ref, bf16[4,1536,256]{2,1,0:T(8,128)(2,1)S(1)} %maximum_bitcast_fusion.kv_ref), custom_call_target="tpu_custom_call" | custom-call | flops 14495514624 | bytes 7864320 | tf_op jit(solution)/shard_map/attend/pallas_call | solution.py:221
  296.4 16.1 %collective-permute-done.1 = bf16[384,1664]{1,0:T(8,128)(2,1)S(1)} collective-permute-done((bf16[384,1664]{1,0:T(8,128)(2,1)S(1)}, bf16[384,1664]{1,0:T(8,128)(2,1)S(1)}, u32[]{:S(2)}, u32[]{:S(2)}) %collective-permute-start.1) | collective-permute-done | bytes 1277984 | tf_op jit(solution)/shard_map/ppermute | solution.py:23
  332.0 33.7 %fusion.16 = f32[3072,2560]{0,1:T(8,128)} fusion(bf16[1536,2560]{0,1:T(8,128)(2,1)} %all-gather.9.cloned.1.call-done, bf16[3072,1664]{1,0:T(8,128)(2,1)} %constant_dynamic-update-slice_fusion), kind=kOutput, calls=%fused_computation.33 | convolution fusion | flops 24159191040 | bytes 48758784 | tf_op jit(solution)/shard_map/dot_general | solution.py:133
  365.8 21.3 %fusion = (bf16[3072,1280]{0,1:T(8,128)(2,1)S(1)}, bf16[3072,1280]{0,1:T(8,128)(2,1)}, f32[3072,1280]{0,1:T(8,128)}) fusion(f32[3072,2560]{0,1:T(8,128)} %fusion.16, s32[1280]{0:T(1024)S(1)} %copy-done.86, s32[1280]{0:T(1024)S(1)} %get-tuple-element.242, bf16[3072,1664]{1,0:T(8,128)(2,1)} %constant_dynamic-update-slice_fusion), kind=kOutput, calls=%fused_computation.2 | convolution fusion | flops 1042513920 | bytes 63711232 | tf_op jit(solution)/shard_map/dot_general | solution.py:133
  390.1 14.2 %convolution_convert_fusion.4 = bf16[1280,1536]{1,0:T(8,128)(2,1)} fusion(bf16[3072,1280]{0,1:T(8,128)(2,1)S(1)} %get-tuple-element.31, bf16[3072,1536]{1,0:T(8,128)(2,1)S(1)} %bitcast.197), kind=kOutput, calls=%fused_computation.30 | convolution fusion | flops 12081561600 | bytes 21233664 | tf_op jit(solution)/shard_map/dot_general | solution.py:137
  404.3 34.7 %multiply_convert_fusion = (bf16[3072,1280]{0,1:T(8,128)(2,1)}, bf16[3072,1280]{0,1:T(8,128)(2,1)}, f32[3072,1280]{0,1:T(8,128)}) fusion(f32[3072,1280]{0,1:T(8,128)} %get-tuple-element.232, f32[3072,2560]{0,1:T(8,128)} %fusion.16, bf16[3072,1536]{1,0:T(8,128)(2,1)} %constant_dynamic-update-slice_fusion.10, bf16[1280,1536]{1,0:T(8,128)(2,1)} %all-gather.11.cloned.1.call-done), kind=kOutput, calls=%fused_computation.6 | convolution fusion | flops 12134645760 | bytes 92012544 | tf_op jit(solution)/shard_map/dot_general | solution.py:129
  438.9 10.8 fusion.62
  449.8 16.9 %fusion.10 = bf16[1536,1536]{1,0:T(8,128)(2,1)S(1)} fusion(bf16[1536,2560]{0,1:T(8,128)(2,1)} %all-gather.9.cloned.1.call-done, bf16[3072,1280]{0,1:T(8,128)(2,1)} %get-tuple-element.150, bf16[3072,1280]{0,1:T(8,128)(2,1)} %get-tuple-element.151), kind=kOutput, calls=%fused_computation.24 | convolution fusion | flops 12097683456 | bytes 28311552 | tf_op jit(solution)/shard_map/dot_general | solution.py:129
  469.8 26.5 %collective-permute-done.27 = bf16[384,1536]{1,0:T(8,128)(2,1)S(1)} collective-permute-done((bf16[384,1536]{1,0:T(8,128)(2,1)S(1)}, bf16[384,1536]{1,0:T(8,128)(2,1)S(1)}, u32[]{:S(2)}, u32[]{:S(2)}) %collective-permute-start.27) | collective-permute-done | bytes 1179680 | tf_op jit(solution)/shard_map/ppermute | solution.py:23
  498.3 17.1 %fusion.11 = bf16[1536,1536]{1,0:T(8,128)(2,1)S(1)} fusion(bf16[1536,2560]{0,1:T(8,128)(2,1)} %all-gather.9.cloned.1.call-done, bf16[3072,1280]{0,1:T(8,128)(2,1)} %get-tuple-element.151, bf16[3072,1280]{0,1:T(8,128)(2,1)} %get-tuple-element.150), kind=kOutput, calls=%fused_computation.25 | convolution fusion | flops 12097683456 | bytes 28311552 | tf_op jit(solution)/shard_map/dot_general | solution.py:129
  535.0 18.1 %convolution_convert_fusion.2 = bf16[1536,1280]{1,0:T(8,128)(2,1)} fusion(bf16[3072,1280]{0,1:T(8,128)(2,1)} %get-tuple-element.150, bf16[3072,1664]{1,0:T(8,128)(2,1)} %constant_dynamic-update-slice_fusion), kind=kOutput, calls=%fused_computation.28 | convolution fusion | flops 12081561600 | bytes 21233664 | tf_op jit(solution)/shard_map/dot_general | solution.py:137
  559.7 18.6 %convolution_convert_fusion.3 = bf16[1536,1280]{1,0:T(8,128)(2,1)} fusion(bf16[3072,1280]{0,1:T(8,128)(2,1)} %get-tuple-element.151, bf16[3072,1664]{1,0:T(8,128)(2,1)} %constant_dynamic-update-slice_fusion), kind=kOutput, calls=%fused_computation.29 | convolution fusion | flops 12081561600 | bytes 21233664 | tf_op jit(solution)/shard_map/dot_general | solution.py:137
  581.9 6.7 copy.493
  606.6 51.1 %attend_back.1 = (f32[4,384,384]{2,1,0:T(8,128)}, bf16[4,1536,256]{2,1,0:T(8,128)(2,1)}) custom-call(bf16[4,384,384]{2,1,0:T(8,128)(2,1)} %copy-done.1, bf16[4,1536,256]{2,1,0:T(8,128)(2,1)} %copy-done, bf16[4,384,384]{2,1,0:T(8,128)(2,1)} %bitcast.190, f32[4,6,384]{2,1,0:T(8,128)} %copy-done.2), custom_call_target="tpu_custom_call" | custom-call | flops 36238786560 | bytes 16515072 | tf_op jit(solution)/shard_map/attend_back/pallas_call | solution.py:244
  687.2 8.6 collective-permute-done.38
  699.6 35.4 %reduce-scatter.16.cloned.1.call-done = bf16[128,1024]{1,0:T(8,128)(2,1)} async-done(((bf16[1024,1024]{1,0:T(8,128)(2,1)}), bf16[128,1024]{1,0:T(8,128)(2,1)}) %reduce-scatter.16.cloned.1.call-update) | async-done | bytes 262160
  756.7 14.7 %collective-permute-done.39 = bf16[2,384,640]{2,1,0:T(8,128)(2,1)S(1)} collective-permute-done((bf16[2,384,640]{2,1,0:T(8,128)(2,1)S(1)}, bf16[2,384,640]{2,1,0:T(8,128)(2,1)S(1)}, u32[]{:S(2)}, u32[]{:S(2)}) %collective-permute-start.39) | collective-permute-done | bytes 983072 | tf_op jit(solution)/shard_map/ppermute | solution.py:23
  773.4 5.5 fusion.45
  783.9 6.0 convolution_convert_fusion.5
  791.9 5.8 copy.530
  797.8 10.7 convolution_convert_fusion
  808.9 9.3 convolution_convert_fusion.1
  822.7 14.2 %collective-permute-done.33 = bf16[192,1536]{1,0:T(8,128)(2,1)S(1)} collective-permute-done((bf16[192,1536]{1,0:T(8,128)(2,1)S(1)}, bf16[192,1536]{1,0:T(8,128)(2,1)S(1)}, u32[]{:S(2)}, u32[]{:S(2)}) %collective-permute-start.33) | collective-permute-done | bytes 589856 | tf_op jit(solution)/shard_map/ppermute | solution.py:23
  839.8 8.9 collective-permute-done.32
  867.7 16.4 %reduce-scatter.14.cloned.1.call-done = bf16[320,1536]{1,0:T(8,128)(2,1)} async-done(((bf16[1280,1536]{1,0:T(8,128)(2,1)}), bf16[320,1536]{1,0:T(8,128)(2,1)}) %reduce-scatter.14.cloned.1.call-update) | async-done | bytes 983056 | tf_op jit(solution)/shard_map/reduce_scatter | solution.py:432
  913.3 57.3 %reduce-scatter.18.cloned.1.call-done = bf16[192,1152]{1,0:T(8,128)(2,1)} async-done(((bf16[1536,1152]{1,0:T(8,128)(2,1)}), bf16[192,1152]{1,0:T(8,128)(2,1)}) %reduce-scatter.18.cloned.1.call-update) | async-done | bytes 442384 | tf_op jit(solution)/shard_map/reduce_scatter | solution.py:507
  972.0 73.1 %reduce-scatter.12.cloned.1.call-done = bf16[384,1280]{1,0:T(8,128)(2,1)} async-done(((bf16[1536,1280]{1,0:T(8,128)(2,1)}), bf16[384,1280]{1,0:T(8,128)(2,1)}) %reduce-scatter.12.cloned.1.call-update) | async-done | bytes 983056 | tf_op jit(solution)/shard_map/reduce_scatter | solution.py:438
  1057.8 6.1 fusion.44
  (515 shorter events, 320.4 us)
Async XLA Ops:
  7.2 110.7 %all-gather.5.cloned.1.call-start = ((), (), s32[]{:S(2)}) async-start(), calls=%async_computation.5 | async-start | bytes 14598144 | tf_op jit(solution)/shard_map/all_gather | solution.py:321
  12.5 229.4 %all-gather.7.cloned.1.call-start = ((), (), s32[]{:S(2)}) async-start(), calls=%async_computation.6 | async-start | bytes 2359296 | tf_op jit(solution)/shard_map/all_gather | solution.py:366
  129.8 202.2 %all-gather.9.cloned.1.call-start = ((), (), s32[]{:S(2)}) async-start(), calls=%async_computation.7 | async-start | bytes 9830400 | tf_op jit(solution)/shard_map/all_gather | solution.py:339
  142.3 33.2 %collective-permute-start.10 = (bf16[192,2560]{1,0:T(8,128)(2,1)}, bf16[192,2560]{1,0:T(8,128)(2,1)}, u32[]{:S(2)}, u32[]{:S(2)}) collective-permute-start(bf16[192,2560]{1,0:T(8,128)(2,1)} %copy.482), channel_id=1, source_target_pairs={{0,1},{1,0},{2,3},{3,2},{4,5},{5,4},{6,7},{7,6},{8,9},{9,8},{10,11... | collective-permute-start | bytes 2949128 | tf_op jit(solution)/shard_map/ppermute | solution.py:23
  182.3 221.9 %all-gather.11.cloned.1.call-start = ((), (), s32[]{:S(2)}) async-start(), calls=%async_computation.8 | async-start | bytes 4915200 | tf_op jit(solution)/shard_map/all_gather | solution.py:340
  182.4 26.9 %collective-permute-start.11 = (bf16[384,1536]{1,0:T(8,128)(2,1)}, bf16[384,1536]{1,0:T(8,128)(2,1)}, u32[]{:S(2)}, u32[]{:S(2)}) collective-permute-start(bf16[384,1536]{1,0:T(8,128)(2,1)} %param.15), channel_id=1, source_target_pairs={{0,1},{1,0},{2,3},{3,2},{4,5},{5,4},{6,7},{7,6},{8,9},{9,8},{10,11... | collective-permute-start | bytes 3538952 | tf_op jit(solution)/shard_map/ppermute | solution.py:23
  184.9 26.7 %collective-permute-start.12 = (bf16[384,1536]{1,0:T(8,128)(2,1)}, bf16[384,1536]{1,0:T(8,128)(2,1)}, u32[]{:S(2)}, u32[]{:S(2)}) collective-permute-start(bf16[384,1536]{1,0:T(8,128)(2,1)} %param.15), channel_id=1, source_target_pairs={{0,16},{16,0},{1,17},{17,1},{2,18},{18,2},{3,19},{19,3},{4,20},{20... | collective-permute-start | bytes 3538952 | tf_op jit(solution)/shard_map/ppermute | solution.py:23
  184.9 102.9 %collective-permute-start.15 = (bf16[384,1536]{1,0:T(8,128)(2,1)}, bf16[384,1536]{1,0:T(8,128)(2,1)}, u32[]{:S(2)}, u32[]{:S(2)}) collective-permute-start(bf16[384,1536]{1,0:T(8,128)(2,1)} %param.15), channel_id=1, source_target_pairs={{0,8},{8,0},{1,9},{9,1},{2,10},{10,2},{3,11},{11,3},{4,12},{12,4},... | collective-permute-start | bytes 3538952 | tf_op jit(solution)/shard_map/ppermute | solution.py:23
  184.9 550.0 %reduce-scatter.16.cloned.1.call-start = ((), (), s32[]{:S(2)}) async-start(), calls=%async_computation.12 | async-start | bytes 2359296
  213.5 71.8 %collective-permute-start.14 = (bf16[192,1536]{1,0:T(8,128)(2,1)}, bf16[192,1536]{1,0:T(8,128)(2,1)}, u32[]{:S(2)}, u32[]{:S(2)}) collective-permute-start(bf16[192,1536]{1,0:T(8,128)(2,1)} %slice.569), channel_id=1, source_target_pairs={{0,1},{1,0},{2,3},{3,2},{4,5},{5,4},{6,7},{7,6},{8,9},{9,8},{10,11... | collective-permute-start | bytes 1769480 | tf_op jit(solution)/shard_map/ppermute | solution.py:23
  214.6 75.6 %collective-permute-start.16 = (bf16[384,1536]{1,0:T(8,128)(2,1)}, bf16[384,1536]{1,0:T(8,128)(2,1)}, u32[]{:S(2)}, u32[]{:S(2)}) collective-permute-start(bf16[384,1536]{1,0:T(8,128)(2,1)} %collective-permute-done.11), channel_id=1, source_target_pairs={{0,8},{8,0},{1,9},{9,1},{2,10},{10,2},{3,11},{11,3},{4,12},{12,4},... | collective-permute-start | bytes 3538952 | tf_op jit(solution)/shard_map/ppermute | solution.py:23
  214.6 78.5 %collective-permute-start.17 = (bf16[384,1536]{1,0:T(8,128)(2,1)}, bf16[384,1536]{1,0:T(8,128)(2,1)}, u32[]{:S(2)}, u32[]{:S(2)}) collective-permute-start(bf16[384,1536]{1,0:T(8,128)(2,1)} %collective-permute-done.12), channel_id=1, source_target_pairs={{0,8},{8,0},{1,9},{9,1},{2,10},{10,2},{3,11},{11,3},{4,12},{12,4},... | collective-permute-start | bytes 3538952 | tf_op jit(solution)/shard_map/ppermute | solution.py:23
  284.6 27.9 %collective-permute-start.1 = (bf16[384,1664]{1,0:T(8,128)(2,1)S(1)}, bf16[384,1664]{1,0:T(8,128)(2,1)S(1)}, u32[]{:S(2)}, u32[]{:S(2)}) collective-permute-start(bf16[384,1664]{1,0:T(8,128)(2,1)S(1)} %get-tuple-element.191), channel_id=1, source_target_pairs={{0,1},{1,0},{2,3},{3,2},{4,5},{5,4},{6,7},{7,6},{8,9},{9,8},{10,11... | collective-permute-start | bytes 3833864 | tf_op jit(solution)/shard_map/ppermute | solution.py:23
  285.3 27.5 %collective-permute-start.2 = (bf16[384,1664]{1,0:T(8,128)(2,1)S(1)}, bf16[384,1664]{1,0:T(8,128)(2,1)S(1)}, u32[]{:S(2)}, u32[]{:S(2)}) collective-permute-start(bf16[384,1664]{1,0:T(8,128)(2,1)S(1)} %get-tuple-element.191), channel_id=1, source_target_pairs={{0,16},{16,0},{1,17},{17,1},{2,18},{18,2},{3,19},{19,3},{4,20},{20... | collective-permute-start | bytes 3833864 | tf_op jit(solution)/shard_map/ppermute | solution.py:23
  290.2 26.2 %collective-permute-start.19 = (bf16[192,1536]{1,0:T(8,128)(2,1)}, bf16[192,1536]{1,0:T(8,128)(2,1)S(1)}, u32[]{:S(2)}, u32[]{:S(2)}) collective-permute-start(bf16[192,1536]{1,0:T(8,128)(2,1)} %collective-permute-done.14), channel_id=1, source_target_pairs={{0,8},{8,0},{1,9},{9,1},{2,10},{10,2},{3,11},{11,3},{4,12},{12,4},... | collective-permute-start | bytes 1769480 | tf_op jit(solution)/shard_map/ppermute | solution.py:23
  295.5 31.3 %collective-permute-start.5 = (bf16[384,1664]{1,0:T(8,128)(2,1)S(1)}, bf16[384,1664]{1,0:T(8,128)(2,1)S(1)}, u32[]{:S(2)}, u32[]{:S(2)}) collective-permute-start(bf16[384,1664]{1,0:T(8,128)(2,1)S(1)} %get-tuple-element.191), channel_id=1, source_target_pairs={{0,8},{8,0},{1,9},{9,1},{2,10},{10,2},{3,11},{11,3},{4,12},{12,4},... | collective-permute-start | bytes 3833864 | tf_op jit(solution)/shard_map/ppermute | solution.py:23
  467.2 48.3 %collective-permute-start.20 = (bf16[1536,1664]{1,0:T(8,128)(2,1)S(1)}, bf16[1536,1664]{1,0:T(8,128)(2,1)S(1)}, u32[]{:S(2)}, u32[]{:S(2)}) collective-permute-start(bf16[1536,1664]{1,0:T(8,128)(2,1)S(1)} %pad_maximum_fusion.4), channel_id=1, source_target_pairs={{0,8},{8,0},{1,9},{9,1},{2,10},{10,2},{3,11},{11,3},{4,12},{12,4},... | collective-permute-start | bytes 15335432 | tf_op jit(solution)/shard_map/ppermute | solution.py:23
  468.0 28.2 %collective-permute-start.27 = (bf16[384,1536]{1,0:T(8,128)(2,1)S(1)}, bf16[384,1536]{1,0:T(8,128)(2,1)S(1)}, u32[]{:S(2)}, u32[]{:S(2)}) collective-permute-start(bf16[384,1536]{1,0:T(8,128)(2,1)S(1)} %copy-done.54), channel_id=1, source_target_pairs={{0,16},{16,0},{1,17},{17,1},{2,18},{18,2},{3,19},{19,3},{4,20},{20... | collective-permute-start | bytes 3538952 | tf_op jit(solution)/shard_map/ppermute | solution.py:23
  497.5 27.4 %collective-permute-start.29 = (bf16[384,1536]{0,1:T(8,128)(2,1)S(1)}, bf16[384,1536]{0,1:T(8,128)(2,1)S(1)}, u32[]{:S(2)}, u32[]{:S(2)}) collective-permute-start(bf16[384,1536]{0,1:T(8,128)(2,1)S(1)} %bitcast.152), channel_id=1, source_target_pairs={{0,16},{16,0},{1,17},{17,1},{2,18},{18,2},{3,19},{19,3},{4,20},{20... | collective-permute-start | bytes 3538952 | tf_op jit(solution)/shard_map/ppermute | solution.py:23
  526.7 51.5 %collective-permute-start.30 = (bf16[2,384,1536]{1,2,0:T(8,128)(2,1)}, bf16[2,384,1536]{1,2,0:T(8,128)(2,1)}, u32[]{:S(2)}, u32[]{:S(2)}) collective-permute-start(bf16[2,384,1536]{1,2,0:T(8,128)(2,1)} %pad_maximum_fusion.9), channel_id=1, source_target_pairs={{0,8},{8,0},{1,9},{9,1},{2,10},{10,2},{3,11},{11,3},{4,12},{12,4},... | collective-permute-start | bytes 7077896 | tf_op jit(solution)/shard_map/ppermute | solution.py:23
  553.1 35.6 %collective-permute-start.21 = (bf16[192,1664]{1,0:T(8,128)(2,1)}, bf16[192,1664]{1,0:T(8,128)(2,1)S(1)}, u32[]{:S(2)}, u32[]{:S(2)}) collective-permute-start(bf16[192,1664]{1,0:T(8,128)(2,1)} %get-tuple-element.155), channel_id=1, source_target_pairs={{0,1},{1,0},{2,3},{3,2},{4,5},{5,4},{6,7},{7,6},{8,9},{9,8},{10,11... | collective-permute-start | bytes 1916936 | tf_op jit(solution)/shard_map/ppermute | solution.py:23
  554.8 33.8 %collective-permute-start.23 = (bf16[192,1664]{1,0:T(8,128)(2,1)}, bf16[192,1664]{1,0:T(8,128)(2,1)}, u32[]{:S(2)}, u32[]{:S(2)}) collective-permute-start(bf16[192,1664]{1,0:T(8,128)(2,1)} %get-tuple-element.156), channel_id=1, source_target_pairs={{0,16},{16,0},{1,17},{17,1},{2,18},{18,2},{3,19},{19,3},{4,20},{20... | collective-permute-start | bytes 1916936 | tf_op jit(solution)/shard_map/ppermute | solution.py:23
  555.1 33.6 %collective-permute-start.24 = (bf16[192,1664]{1,0:T(8,128)(2,1)}, bf16[192,1664]{1,0:T(8,128)(2,1)}, u32[]{:S(2)}, u32[]{:S(2)}) collective-permute-start(bf16[192,1664]{1,0:T(8,128)(2,1)} %get-tuple-element.154), channel_id=1, source_target_pairs={{0,16},{16,0},{1,17},{17,1},{2,18},{18,2},{3,19},{19,3},{4,20},{20... | collective-permute-start | bytes 1916936 | tf_op jit(solution)/shard_map/ppermute | solution.py:23
  559.4 29.3 %collective-permute-start.26 = (bf16[192,1664]{1,0:T(8,128)(2,1)}, bf16[192,1664]{1,0:T(8,128)(2,1)}, u32[]{:S(2)}, u32[]{:S(2)}) collective-permute-start(bf16[192,1664]{1,0:T(8,128)(2,1)} %add_convert_fusion), channel_id=1, source_target_pairs={{0,1},{1,0},{2,3},{3,2},{4,5},{5,4},{6,7},{7,6},{8,9},{9,8},{10,11... | collective-permute-start | bytes 1916936 | tf_op jit(solution)/shard_map/ppermute | solution.py:23
  668.7 196.3 %reduce-scatter.10.cloned.1.call-start = ((), (), s32[]{:S(2)}) async-start(), calls=%async_computation.9 | async-start | bytes 4915200 | tf_op jit(solution)/shard_map/reduce_scatter | solution.py:438
  669.3 214.9 %reduce-scatter.14.cloned.1.call-start = ((), (), s32[]{:S(2)}) async-start(), calls=%async_computation.11 | async-start | bytes 4915200 | tf_op jit(solution)/shard_map/reduce_scatter | solution.py:432
  670.0 300.5 %reduce-scatter.18.cloned.1.call-start = ((), (), s32[]{:S(2)}) async-start(), calls=%async_computation.13 | async-start | bytes 3981312 | tf_op jit(solution)/shard_map/reduce_scatter | solution.py:507
  699.6 52.8 %collective-permute-start.42 = (bf16[2,384,384]{2,1,0:T(8,128)(2,1)}, bf16[2,384,384]{2,1,0:T(8,128)(2,1)}, u32[]{:S(2)}, u32[]{:S(2)}) collective-permute-start(bf16[2,384,384]{2,1,0:T(8,128)(2,1)} %pad_maximum_fusion.25), channel_id=1, source_target_pairs={{0,8},{8,0},{1,9},{9,1},{2,10},{10,2},{3,11},{11,3},{4,12},{12,4},... | collective-permute-start | bytes 1769480 | tf_op jit(solution)/shard_map/ppermute | solution.py:23
  797.7 247.4 %reduce-scatter.12.cloned.1.call-start = ((), (), s32[]{:S(2)}) async-start(), calls=%async_computation.10 | async-start | bytes 4915200 | tf_op jit(solution)/shard_map/reduce_scatter | solution.py:438
  821.6 27.1 %collective-permute-start.32 = (bf16[192,1536]{1,0:T(8,128)(2,1)S(1)}, bf16[192,1536]{1,0:T(8,128)(2,1)S(1)}, u32[]{:S(2)}, u32[]{:S(2)}) collective-permute-start(bf16[192,1536]{1,0:T(8,128)(2,1)S(1)} %get-tuple-element.161), channel_id=1, source_target_pairs={{0,1},{1,0},{2,3},{3,2},{4,5},{5,4},{6,7},{7,6},{8,9},{9,8},{10,11... | collective-permute-start | bytes 1769480 | tf_op jit(solution)/shard_map/ppermute | solution.py:23
  855.2 33.3 %collective-permute-start.36 = (bf16[192,1536]{1,0:T(8,128)(2,1)}, bf16[192,1536]{1,0:T(8,128)(2,1)}, u32[]{:S(2)}, u32[]{:S(2)}) collective-permute-start(bf16[192,1536]{1,0:T(8,128)(2,1)} %get-tuple-element.159), channel_id=1, source_target_pairs={{0,16},{16,0},{1,17},{17,1},{2,18},{18,2},{3,19},{19,3},{4,20},{20... | collective-permute-start | bytes 1769480 | tf_op jit(solution)/shard_map/ppermute | solution.py:23
  970.5 80.2 %collective-permute-start.43 = (bf16[192,1152]{1,0:T(8,128)(2,1)}, bf16[192,1152]{1,0:T(8,128)(2,1)}, u32[]{:S(2)}, u32[]{:S(2)}) collective-permute-start(bf16[192,1152]{1,0:T(8,128)(2,1)} %reduce-scatter.18.cloned.1.call-done), channel_id=1, source_target_pairs={{0,16},{16,0},{1,17},{17,1},{2,18},{18,2},{3,19},{19,3},{4,20},{20... | collective-permute-start | bytes 1327112 | tf_op jit(solution)/shard_map/ppermute | solution.py:23
  (131 other events, 2493.1 us)
Sparse Core Ops, SparseCore 0:
  12.6 105.2 all-gather.4
  130.0 56.4 all-gather.6
  188.7 139.3 all-gather.8
  329.5 74.5 all-gather.10
  668.8 66.0 reduce-scatter.15
  737.1 71.6 reduce-scatter.9
  811.1 73.0 reduce-scatter.13
  887.8 82.6 reduce-scatter.17
  972.8 72.2 reduce-scatter.11
